TPU v7x, 256 devices: a whole 4x4x8 slice. The times are simulated.
256 devices in a mesh: gx: 8 (over x, core), gy: 4 (over y), gz: 8 (over z).
Axes of the slice: x: 4, y: 4, z: 8, core: 2. Of those that a mesh axis runs over, the one named last changes fastest.
Arguments:
- velocity: float32 [3, 128, 128, 1024], P(None, 'gx', 'gy', 'gz'), may hold values from -6 to 6
- forcing: float32 [3, 128, 128, 1024], P(None, 'gx', 'gy', 'gz'), may hold values from -12 to 12
- phase_block: int32 [32, 32, 256], P('gx', 'gy', 'gz'), may hold values from 0 to 7
- prefactor: float32 [8], replicated, may hold values from 0.5 to 4
- yield_stress: float32 [8], replicated, may hold values from 1 to 16
Outputs:
- smoothed: float32 [3, 128, 128, 1024], P(None, 'gx', 'gy', 'gz')
- viscosity_field: float32 [128, 128, 1024], P('gx', 'gy', 'gz')
- coarse_one: float32 [64, 64, 512], P('gx', 'gy', 'gz')
- coarse_two: float32 [32, 32, 256], P('gx', 'gy', 'gz')
- coarse_three: float32 [16, 16, 128], P('gx', 'gy', 'gz')
- residual_field: float32 [3, 128, 128, 1024], P(None, 'gx', 'gy', 'gz')
- residual_rms: float32 [], replicated
All inputs are finite; a program needn't handle non-finite values.
Results may differ from a plain program's by a relative error of at most 0.000053.
Values sent between devices are 32-bit elements; how exact they have to be, the bound alone decides.
A program may use at most 64 MiB of HBM per device.

v0:
```python
import functools

import jax
import jax.numpy as jnp
from jax import lax
from jax.sharding import Mesh
from jax.sharding import PartitionSpec as P

BLOCK = 4
GX = ("gx_0", "gx_1")
GX_GY_GZ = ("gx_0", "gx_1", "gy", "gz")


RELAXATION = 0.8
NEIGHBOUR_OFFSETS = ((1, 0, 0), (-1, 0, 0), (0, 1, 0), (0, -1, 0), (0, 0, 1), (0, 0, -1))
UNIT_STEPS = ((1, 0, 0), (0, 1, 0), (0, 0, 1))


def padded_2(shard, sides, width):
    edges = {}
    for axis, dim in sides:
        peers, length = (lax.axis_size(axis), shard.shape[dim])
        up = [(i, (i + 1) % peers) for i in range(peers - 1)]
        last = lax.slice_in_dim(shard, length - width, length, axis=dim)
        initial = lax.slice_in_dim(shard, 0, width, axis=dim)
        edges[dim] = (
            lax.ppermute(last, axis, up),
            lax.ppermute(initial, axis, [(b, a) for a, b in up]),
        )
    done = []
    for _, dim in sides:
        low, high = edges[dim]
        around = [(width, width) if d in done else (0, 0) for d in range(shard.ndim)]
        shard = jnp.concatenate([jnp.pad(low, around), shard, jnp.pad(high, around)], axis=dim)
        done.append(dim)
    return shard


def by_axis(shard, axes):
    return functools.reduce(lax.psum, axes, shard)


def padded_3(block, sides, width):
    for axis, dim in sides:
        count = lax.axis_size(axis)
        forward = [(i, i + 1) for i in range(count - 1)]
        backward = [(target, source) for source, target in forward]
        low = lax.ppermute(
            lax.slice_in_dim(block, block.shape[dim] - width, None, axis=dim), axis, forward
        )
        high = lax.ppermute(lax.slice_in_dim(block, 0, width, axis=dim), axis, backward)
        block = jnp.concatenate([low, block, high], axis=dim)
    return block


def offset_view(field, shift_x, shift_y, shift_z):
    size_x = field.shape[-3] - 2
    size_y = field.shape[-2] - 2
    size_z = field.shape[-1] - 2
    return field[
        ...,
        1 + shift_x : 1 + shift_x + size_x,
        1 + shift_y : 1 + shift_y + size_y,
        1 + shift_z : 1 + shift_z + size_z,
    ]


def viscosity_of(padded_vel, prefactor_cells, yield_cells):
    gradient = []
    for comp_a in range(3):
        row_list = []
        for comp_b in range(3):
            step_up = UNIT_STEPS[comp_b]
            step_down = (-step_up[0], -step_up[1], -step_up[2])
            row_list.append(
                0.5
                * (
                    offset_view(padded_vel[comp_a], *step_up)
                    - offset_view(padded_vel[comp_a], *step_down)
                )
            )
        gradient.append(row_list)
    strain_sq = jnp.zeros(gradient[0][0].shape, jnp.float32)
    for comp_a in range(3):
        for comp_b in range(3):
            strain = 0.5 * (gradient[comp_a][comp_b] + gradient[comp_b][comp_a])
            strain_sq = strain_sq + strain * strain
    invariant = 0.5 * strain_sq + 1.0
    creeping = prefactor_cells * jnp.power(invariant, -1.0 / 3.0)
    plastic = yield_cells / (2.0 * jnp.sqrt(invariant))
    return jnp.minimum(creeping, plastic)


def restrict_dim(field, dim_index):
    coarse_len = (field.shape[dim_index] - 2) // 2

    def every_other(start):
        return lax.slice_in_dim(field, start, start + 2 * coarse_len - 1, 2, dim_index)

    return (every_other(0) + 3.0 * every_other(1) + 3.0 * every_other(2) + every_other(3)) * 0.125


def coarsen(padded):
    return restrict_dim(restrict_dim(restrict_dim(padded, 0), 1), 2)


def smooth_terms(padded_vel, padded_visc):
    centre = offset_view(padded_visc, 0, 0, 0)
    diagonal = jnp.zeros(centre.shape, jnp.float32)
    neighbours = jnp.zeros((3,) + centre.shape, jnp.float32)
    for offset in NEIGHBOUR_OFFSETS:
        face_visc = 0.5 * (centre + offset_view(padded_visc, *offset))
        diagonal = diagonal + face_visc
        neighbours = neighbours + face_visc[None] * offset_view(padded_vel, *offset)
    return (diagonal, neighbours)


def jacobi_sweep(padded_vel, padded_visc, forcing):
    diagonal, neighbours = smooth_terms(padded_vel, padded_visc)
    centre_vel = offset_view(padded_vel, 0, 0, 0)
    return (
        centre_vel
        + RELAXATION * (forcing - (diagonal[None] * centre_vel - neighbours)) / diagonal[None]
    )


def misfit(padded_vel, padded_visc, forcing):
    diagonal, neighbours = smooth_terms(padded_vel, padded_visc)
    centre_vel = offset_view(padded_vel, 0, 0, 0)
    return forcing - (diagonal[None] * centre_vel - neighbours)


def expand_table(phase_block, table):
    block_table = jnp.zeros(phase_block.shape, jnp.float32)
    for phase_id in range(table.shape[0]):
        block_table = block_table + jnp.where(phase_block == phase_id, table[phase_id], 0.0)
    blocks_x, blocks_y, blocks_z = phase_block.shape
    spread = jnp.broadcast_to(
        block_table[:, None, :, None, :, None], (blocks_x, BLOCK, blocks_y, BLOCK, blocks_z, BLOCK)
    )
    return spread.reshape(blocks_x * BLOCK, blocks_y * BLOCK, blocks_z * BLOCK)


def inside_box(box_shape, rim_width, block_cells):
    along_x = lax.iota(jnp.int32, box_shape[0]) + lax.axis_index(GX) * block_cells[0] - rim_width
    along_y = lax.iota(jnp.int32, box_shape[1]) + lax.axis_index("gy") * block_cells[1] - rim_width
    along_z = lax.iota(jnp.int32, box_shape[2]) + lax.axis_index("gz") * block_cells[2] - rim_width
    inside_x = (along_x >= 0) & (along_x < block_cells[0] * lax.axis_size(GX))
    inside_y = (along_y >= 0) & (along_y < block_cells[1] * lax.axis_size("gy"))
    inside_z = (along_z >= 0) & (along_z < block_cells[2] * lax.axis_size("gz"))
    return inside_x[:, None, None] & inside_y[None, :, None] & inside_z[None, None, :]


def sweep_halo(field):
    return padded_2(field, ((GX, 1), ("gy", 2), ("gz", 3)), 1)


def per_device(velocity, forcing, phase_block, prefactor, yield_stress):
    cells_x, cells_y, cells_z = (velocity.shape[1], velocity.shape[2], velocity.shape[3])
    block_cells = (cells_x, cells_y, cells_z)
    prefactor_cells = expand_table(phase_block, prefactor)
    yield_cells = expand_table(phase_block, yield_stress)
    padded_vel = sweep_halo(velocity)
    viscosity_field = viscosity_of(padded_vel, prefactor_cells, yield_cells)
    padded_visc = padded_2(viscosity_field, ((GX, 0), ("gy", 1), ("gz", 2)), 1)
    current = jacobi_sweep(padded_vel, padded_visc, forcing)
    current = jacobi_sweep(sweep_halo(current), padded_visc, forcing)
    padded_final = padded_2(current, ((GX, 1), ("gy", 2), ("gz", 3)), 1)
    misfit_field = misfit(padded_final, padded_visc, forcing)
    sum_squares = by_axis(jnp.sum(misfit_field * misfit_field), GX_GY_GZ)
    all_cells = float(
        3
        * cells_x
        * lax.axis_size(GX)
        * cells_y
        * lax.axis_size("gy")
        * cells_z
        * lax.axis_size("gz")
    )
    residual_rms = jnp.sqrt(sum_squares / all_cells)
    levels = []
    level_field = padded_3(viscosity_field, ((GX, 0), ("gy", 1), ("gz", 2)), 7)
    rim_width = 7
    level_cells = block_cells
    for level in range(3):
        level_field = coarsen(level_field)
        rim_width = (rim_width - 1) // 2
        level_cells = (level_cells[0] // 2, level_cells[1] // 2, level_cells[2] // 2)
        level_field = jnp.where(
            inside_box(level_field.shape, rim_width, level_cells), level_field, 0.0
        )
        levels.append(
            level_field[
                rim_width : level_field.shape[0] - rim_width,
                rim_width : level_field.shape[1] - rim_width,
                rim_width : level_field.shape[2] - rim_width,
            ]
        )
    return (current, viscosity_field, levels[0], levels[1], levels[2], misfit_field, residual_rms)


def solution(mesh):
    split = Mesh(
        mesh.devices.reshape(4, 2, mesh.shape["gy"], mesh.shape["gz"]), ("gx_0", "gx_1", "gy", "gz")
    )
    return jax.shard_map(
        per_device,
        mesh=split,
        in_specs=(P(None, GX, "gy", "gz"), P(None, GX, "gy", "gz"), P(GX, "gy", "gz"), P(), P()),
        out_specs=(
            P(None, GX, "gy", "gz"),
            P(GX, "gy", "gz"),
            P(GX, "gy", "gz"),
            P(GX, "gy", "gz"),
            P(GX, "gy", "gz"),
            P(None, GX, "gy", "gz"),
            P(),
        ),
        check_vma=False,
    )
```

profile of v0, /device:TPU:8, one launch (start us, length us, event | category | flops | bytes accessed | tf_op | source)
XLA Modules:
  0.0 232.8 jit_solution(3585826509020688203)
XLA Ops:
  6.5 3.8 %collective-permute-start = (f32[3,16,32,1]{2,1,3,0:T(8,128)S(1)}, f32[3,16,32,1]{2,1,3,0:T(8,128)S(1)}, u32[]{:S(2)}, u32[]{:S(2)}) collective-permute-start(f32[3,16,32,1]{2,1,3,0:T(8,128)S(1)} %copy.28), channel_id=1, source_target_pairs={{0,1},{1,2},{2,3},{3,4},{4,5},{5,6},{6,7},{8,9},{9,10},{10,11},{11... | collective-permute-start | bytes 18440 | tf_op jit(solution)/shard_map/ppermute | solution.py:27
  12.0 3.5 %collective-permute-start.1 = (f32[3,16,1,128]{3,2,1,0:T(1,128)S(1)}, f32[3,16,1,128]{3,2,1,0:T(1,128)S(1)}, u32[]{:S(2)}, u32[]{:S(2)}) collective-permute-start(f32[3,16,1,128]{3,2,1,0:T(1,128)S(1)} %get-tuple-element.42), channel_id=1, source_target_pairs={{0,8},{8,16},{16,24},{1,9},{9,17},{17,25},{2,10},{10,18},{18,26},{... | collective-permute-start | bytes 73736 | tf_op jit(solution)/shard_map/ppermute | solution.py:27
  15.5 2.4 %collective-permute-start.4 = (f32[3,16,1,128]{3,2,1,0:T(1,128)S(1)}, f32[3,16,1,128]{3,2,1,0:T(1,128)S(1)}, u32[]{:S(2)}, u32[]{:S(2)}) collective-permute-start(f32[3,16,1,128]{3,2,1,0:T(1,128)S(1)} %get-tuple-element.43), channel_id=1, source_target_pairs={{8,0},{16,8},{24,16},{9,1},{17,9},{25,17},{10,2},{18,10},{26,18},{... | collective-permute-start | bytes 73736 | tf_op jit(solution)/shard_map/ppermute | solution.py:28
  21.2 5.0 %select_add_fusion.1 = (f32[4,8,32]{2,1,0:T(8,128)S(1)}, pred[4,8,32]{2,1,0:T(8,128)(4,1)S(1)}, pred[4,8,32]{2,1,0:T(8,128)(4,1)S(1)}, pred[4,8,32]{2,1,0:T(8,12...) fusion(f32[]{:T(128)} %bitcast.7, f32[]{:T(128)} %bitcast.6, ...), kind=kLoop, calls=%fused_computation.188 | loop fusion | flops 23552 | bytes 16416 | tf_op jit(solution)/shard_map/add | solution.py:136
  26.2 5.0 %select_add_fusion = f32[4,8,32]{2,1,0:T(8,128)S(1)} fusion(pred[4,8,32]{2,1,0:T(8,128)(4,1)S(1)} %get-tuple-element.24, pred[4,8,32]{2,1,0:T(8,128)(4,1)S(1)} %get-tuple-element.23, pred[4,8,32]{2,1,0:T(8,128)(4,1)S(1)} %get-tuple-element.22, pred[4,8,32]{2,1,0:T(8,128)(4,1)S(1)} %get-tuple-element.21, pred[4,8,32]{2,1,0:T(8,128)(4,1)S(1)} %get-tuple-element.20, ...), kind=kLoop, calls=%fused_computation.187 | loop fusion | flops 15360 | bytes 12320 | tf_op jit(solution)/shard_map/add | solution.py:136
  31.8 4.4 %broadcast_in_dim.142 = f32[4,4,8,4,32,4]{5,4,3,2,1,0:T(8,128)} broadcast(f32[4,8,32]{2,1,0:T(8,128)S(1)} %select_add_fusion), dimensions={0,2,4} | broadcast | bytes 266240 | tf_op jit(solution)/shard_map/broadcast_in_dim | solution.py:138
  36.2 8.2 %reshape.195 = f32[16,32,128]{2,1,0:T(8,128)S(1)} reshape(f32[4,4,8,4,32,4]{5,4,3,2,1,0:T(8,128)} %broadcast_in_dim.142) | data formatting | bytes 524288 | tf_op jit(solution)/shard_map/reshape | solution.py:141
  44.4 4.4 %broadcast_in_dim.133 = f32[4,4,8,4,32,4]{5,4,3,2,1,0:T(8,128)} broadcast(f32[4,8,32]{2,1,0:T(8,128)S(1)} %get-tuple-element.16), dimensions={0,2,4} | broadcast | bytes 266240 | tf_op jit(solution)/shard_map/broadcast_in_dim | solution.py:138
  48.8 8.2 %reshape.194 = f32[16,32,128]{2,1,0:T(8,128)S(1)} reshape(f32[4,4,8,4,32,4]{5,4,3,2,1,0:T(8,128)} %broadcast_in_dim.133) | data formatting | bytes 524288 | tf_op jit(solution)/shard_map/reshape | solution.py:141
  66.4 5.2 %collective-permute-start.11 = (f32[16,32,1]{2,1,0:T(8,128)S(1)}, f32[16,32,1]{2,1,0:T(8,128)S(1)}, u32[]{:S(2)}, u32[]{:S(2)}) collective-permute-start(f32[16,32,1]{2,1,0:T(8,128)S(1)} %get-tuple-element.52), channel_id=1, source_target_pairs={{0,1},{1,2},{2,3},{3,4},{4,5},{5,6},{6,7},{8,9},{9,10},{10,11},{11... | collective-permute-start | bytes 6152 | tf_op jit(solution)/shard_map/ppermute | solution.py:27
  72.9 4.8 %collective-permute-start.7 = (f32[1,32,128]{2,1,0:T(8,128)S(1)}, f32[1,32,128]{2,1,0:T(8,128)S(1)}, u32[]{:S(2)}, u32[]{:S(2)}) collective-permute-start(f32[1,32,128]{2,1,0:T(8,128)S(1)} %get-tuple-element.56), channel_id=1, source_target_pairs={{0,32},{32,64},{64,96},{96,128},{128,160},{160,192},{192,224},{1,3... | collective-permute-start | bytes 49160 | tf_op jit(solution)/shard_map/ppermute | solution.py:27
  77.7 3.8 %collective-permute-start.9 = (f32[16,1,128]{2,1,0:T(1,128)S(1)}, f32[16,1,128]{2,1,0:T(1,128)S(1)}, u32[]{:S(2)}, u32[]{:S(2)}) collective-permute-start(f32[16,1,128]{2,1,0:T(1,128)S(1)} %get-tuple-element.54), channel_id=1, source_target_pairs={{0,8},{8,16},{16,24},{1,9},{9,17},{17,25},{2,10},{10,18},{18,26},{... | collective-permute-start | bytes 24584 | tf_op jit(solution)/shard_map/ppermute | solution.py:27
  83.7 4.0 %fusion.39 = f32[3,16,32,128]{3,2,1,0:T(8,128)S(1)} fusion(f32[3,16,32,128]{3,2,1,0:T(8,128)S(1)} %copy-done.2, f32[3,16,32,128]{3,2,1,0:T(8,128)} %param.6, f32[3,18,34,1]{3,2,1,0:T(8,128)S(1)} %pad.52, f32[3,18,1,128]{3,2,1,0:T(1,128)S(1)} %pad.54, f32[3,18,32,128]{3,2,1,0:T(8,128)} %copy-done.14, f32[3,18,1,128]{3,2,1,0:T(1,128)S(1)} %pad.53, ...), kind=kLoop, calls=%fused_computation.80 | loop fusion | flops 5308416 | bytes 5247328 | tf_op jit(solution)/shard_map/add | solution.py:122
  91.4 4.5 %collective-permute-start.17 = (f32[3,16,32,1]{2,1,3,0:T(8,128)S(1)}, f32[3,16,32,1]{2,1,3,0:T(8,128)S(1)}, u32[]{:S(2)}, u32[]{:S(2)}) collective-permute-start(f32[3,16,32,1]{2,1,3,0:T(8,128)S(1)} %copy.18), channel_id=1, source_target_pairs={{0,1},{1,2},{2,3},{3,4},{4,5},{5,6},{6,7},{8,9},{9,10},{10,11},{11... | collective-permute-start | bytes 18440 | tf_op jit(solution)/shard_map/ppermute | solution.py:27
  97.3 3.7 %collective-permute-start.13 = (f32[3,1,32,128]{3,2,1,0:T(8,128)}, f32[3,1,32,128]{3,2,1,0:T(8,128)}, u32[]{:S(2)}, u32[]{:S(2)}) collective-permute-start(f32[3,1,32,128]{3,2,1,0:T(8,128)} %get-tuple-element.36), channel_id=1, source_target_pairs={{0,32},{32,64},{64,96},{96,128},{128,160},{160,192},{192,224},{1,3... | collective-permute-start | bytes 147464 | tf_op jit(solution)/shard_map/ppermute | solution.py:27
  102.9 3.9 %collective-permute-start.15 = (f32[3,16,1,128]{3,2,1,0:T(1,128)}, f32[3,16,1,128]{3,2,1,0:T(1,128)S(1)}, u32[]{:S(2)}, u32[]{:S(2)}) collective-permute-start(f32[3,16,1,128]{3,2,1,0:T(1,128)} %get-tuple-element.38), channel_id=1, source_target_pairs={{0,8},{8,16},{16,24},{1,9},{9,17},{17,25},{2,10},{10,18},{18,26},{... | collective-permute-start | bytes 73736 | tf_op jit(solution)/shard_map/ppermute | solution.py:27
  109.4 3.2 %fusion.22 = f32[3,16,32,128]{3,2,1,0:T(8,128)S(1)} fusion(f32[3,16,32,128]{3,2,1,0:T(8,128)S(1)} %fusion.39, f32[3,16,32,128]{3,2,1,0:T(8,128)S(1)} %copy-done.4, f32[3,16,32,1]{3,2,1,0:T(8,128)} %copy.19, f32[3,18,1,128]{3,2,1,0:T(1,128)S(1)} %pad.60, f32[3,18,1,128]{3,2,1,0:T(1,128)S(1)} %pad.61, f32[3,1,32,128]{3,2,1,0:T(8,128)S(1)} %collective-permute-done.12, ...), kind=kLoop, calls=%fused_computation.43 | loop fusion | flops 8060928 | bytes 4360192 | tf_op jit(solution)/shard_map/add | solution.py:122
  118.9 5.6 %collective-permute-start.29 = (f32[3,16,32,1]{2,1,3,0:T(8,128)S(1)}, f32[3,16,32,1]{2,1,3,0:T(8,128)S(1)}, u32[]{:S(2)}, u32[]{:S(2)}) collective-permute-start(f32[3,16,32,1]{2,1,3,0:T(8,128)S(1)} %copy.26), channel_id=1, source_target_pairs={{0,1},{1,2},{2,3},{3,4},{4,5},{5,6},{6,7},{8,9},{9,10},{10,11},{11... | collective-permute-start | bytes 18440 | tf_op jit(solution)/shard_map/ppermute | solution.py:27
  125.8 3.6 %collective-permute-start.25 = (f32[3,1,32,128]{3,2,1,0:T(8,128)}, f32[3,1,32,128]{3,2,1,0:T(8,128)}, u32[]{:S(2)}, u32[]{:S(2)}) collective-permute-start(f32[3,1,32,128]{3,2,1,0:T(8,128)} %get-tuple-element.32), channel_id=1, source_target_pairs={{0,32},{32,64},{64,96},{96,128},{128,160},{160,192},{192,224},{1,3... | collective-permute-start | bytes 147464 | tf_op jit(solution)/shard_map/ppermute | solution.py:27
  131.3 3.9 %collective-permute-start.27 = (f32[3,16,1,128]{3,2,1,0:T(1,128)}, f32[3,16,1,128]{3,2,1,0:T(1,128)}, u32[]{:S(2)}, u32[]{:S(2)}) collective-permute-start(f32[3,16,1,128]{3,2,1,0:T(1,128)} %get-tuple-element.30), channel_id=1, source_target_pairs={{0,8},{8,16},{16,24},{1,9},{9,17},{17,25},{2,10},{10,18},{18,26},{... | collective-permute-start | bytes 73736 | tf_op jit(solution)/shard_map/ppermute | solution.py:27
  137.2 2.7 %collective-permute-start.18 = (f32[7,32,128]{2,1,0:T(8,128)}, f32[7,32,128]{2,1,0:T(8,128)}, u32[]{:S(2)}, u32[]{:S(2)}) collective-permute-start(f32[7,32,128]{2,1,0:T(8,128)} %get-tuple-element.50), channel_id=1, source_target_pairs={{0,32},{32,64},{64,96},{96,128},{128,160},{160,192},{192,224},{1,3... | collective-permute-start | bytes 344072 | tf_op jit(solution)/shard_map/ppermute | solution.py:48
  144.1 4.4 %multiply_reduce_fusion = (f32[]{:T(128)}, f32[3,16,32,128]{3,2,1,0:T(8,128)}) fusion(f32[3,16,32,128]{3,2,1,0:T(8,128)S(1)} %copy-done.4, f32[3,18,1,128]{3,2,1,0:T(1,128)S(1)} %pad.64, f32[3,1,32,128]{3,2,1,0:T(8,128)S(1)} %collective-permute-done.24, f32[3,16,32,128]{3,2,1,0:T(8,128)S(1)} %fusion.22, f32[3,1,32,128]{3,2,1,0:T(8,128)} %collective-permute-done.25, ...), kind=kLoop, calls=%fused_computation.99 | loop fusion | flops 7864319 | bytes 4360196 | tf_op jit(solution)/shard_map/reduce_sum | solution.py:170
  148.5 11.8 %psum.28 = f32[]{:T(128)} all-reduce(f32[]{:T(128)} %get-tuple-element.7), channel_id=1, replica_groups=mesh['gx_0'=4,'gx_1'=2,'gy'=4,'gz'=8] {'gx_0'}, use_global_device_ids=true, to_apply=%region_1.2 | all-reduce | flops 1 | bytes 8 | tf_op jit(solution)/shard_map/psum | solution.py:40
  161.1 4.2 %collective-permute-start.20 = (f32[30,7,128]{2,1,0:T(8,128)S(1)}, f32[30,7,128]{2,1,0:T(8,128)S(1)}, u32[]{:S(2)}, u32[]{:S(2)}) collective-permute-start(f32[30,7,128]{2,1,0:T(8,128)S(1)} %get-tuple-element.48), channel_id=1, source_target_pairs={{0,8},{8,16},{16,24},{1,9},{9,17},{17,25},{2,10},{10,18},{18,26},{... | collective-permute-start | bytes 322568 | tf_op jit(solution)/shard_map/ppermute | solution.py:48
  167.2 3.1 %psum.29 = f32[]{:T(128)} all-reduce(f32[]{:T(128)} %psum.28), channel_id=1, replica_groups=mesh['gx_0'=4,'gx_1'=2,'gy'=4,'gz'=8] {'gx_1'}, use_global_device_ids=true, to_apply=%region_2.3 | all-reduce | flops 1 | bytes 8 | tf_op jit(solution)/shard_map/psum | solution.py:40
  170.3 9.7 %psum.30 = f32[]{:T(128)} all-reduce(f32[]{:T(128)} %psum.29), channel_id=1, replica_groups=mesh['gx_0'=4,'gx_1'=2,'gy'=4,'gz'=8] {'gy'}, use_global_device_ids=true, to_apply=%region_3.4 | all-reduce | flops 1 | bytes 8 | tf_op jit(solution)/shard_map/psum | solution.py:40
  181.8 4.9 %collective-permute-start.22 = (f32[30,46,7]{1,0,2:T(8,128)S(1)}, f32[30,46,7]{1,0,2:T(8,128)S(1)}, u32[]{:S(2)}, u32[]{:S(2)}) collective-permute-start(f32[30,46,7]{1,0,2:T(8,128)S(1)} %copy.20), channel_id=1, source_target_pairs={{0,1},{1,2},{2,3},{3,4},{4,5},{5,6},{6,7},{8,9},{9,10},{10,11},{11... | collective-permute-start | bytes 115928 | tf_op jit(solution)/shard_map/ppermute | solution.py:48
  188.3 20.7 %psum.31 = f32[]{:T(128)} all-reduce(f32[]{:T(128)} %psum.30), channel_id=1, replica_groups=mesh['gx_0'=4,'gx_1'=2,'gy'=4,'gz'=8] {'gz'}, use_global_device_ids=true, to_apply=%region_4.5 | all-reduce | flops 1 | bytes 8 | tf_op jit(solution)/shard_map/psum | solution.py:40
  214.5 3.1 %slice.525 = f32[14,22,70]{2,1,0:T(8,128)S(1)} slice(f32[14,22,142]{2,1,0:T(8,128)S(1)} %add_multiply_fusion.1), slice={[0:14:1], [0:22:1], [0:139:2]} | slice | bytes 172480 | tf_op jit(solution)/shard_map/slice | solution.py:98
  217.7 3.2 %slice.526 = f32[14,22,70]{2,1,0:T(8,128)S(1)} slice(f32[14,22,142]{2,1,0:T(8,128)S(1)} %add_multiply_fusion.1), slice={[0:14:1], [0:22:1], [1:140:2]} | slice | bytes 172480 | tf_op jit(solution)/shard_map/slice | solution.py:98
  220.9 3.2 %slice.527 = f32[14,22,70]{2,1,0:T(8,128)S(1)} slice(f32[14,22,142]{2,1,0:T(8,128)S(1)} %add_multiply_fusion.1), slice={[0:14:1], [0:22:1], [2:141:2]} | slice | bytes 172480 | tf_op jit(solution)/shard_map/slice | solution.py:98
  224.0 3.2 %slice.528 = f32[14,22,70]{2,1,0:T(8,128)S(1)} slice(f32[14,22,142]{2,1,0:T(8,128)S(1)} %add_multiply_fusion.1), slice={[0:14:1], [0:22:1], [3:142:2]} | slice | bytes 172480 | tf_op jit(solution)/shard_map/slice | solution.py:98
  (188 shorter events, 64.1 us)
Async XLA Ops:
  2.1 57.2 %collective-permute-start.2 = (f32[3,1,32,128]{3,2,1,0:T(8,128)}, f32[3,1,32,128]{3,2,1,0:T(8,128)}, u32[]{:S(2)}, u32[]{:S(2)}) collective-permute-start(f32[3,1,32,128]{3,2,1,0:T(8,128)} %get-tuple-element.45), channel_id=1, source_target_pairs={{0,32},{32,64},{64,96},{96,128},{128,160},{160,192},{192,224},{1,3... | collective-permute-start | bytes 147464 | tf_op jit(solution)/shard_map/ppermute | solution.py:27
  6.5 50.5 %collective-permute-start = (f32[3,16,32,1]{2,1,3,0:T(8,128)S(1)}, f32[3,16,32,1]{2,1,3,0:T(8,128)S(1)}, u32[]{:S(2)}, u32[]{:S(2)}) collective-permute-start(f32[3,16,32,1]{2,1,3,0:T(8,128)S(1)} %copy.28), channel_id=1, source_target_pairs={{0,1},{1,2},{2,3},{3,4},{4,5},{5,6},{6,7},{8,9},{9,10},{10,11},{11... | collective-permute-start | bytes 18440 | tf_op jit(solution)/shard_map/ppermute | solution.py:27
  10.7 48.1 %collective-permute-start.5 = (f32[3,16,32,1]{2,1,3,0:T(8,128)S(1)}, f32[3,16,32,1]{2,1,3,0:T(8,128)S(1)}, u32[]{:S(2)}, u32[]{:S(2)}) collective-permute-start(f32[3,16,32,1]{2,1,3,0:T(8,128)S(1)} %copy.29), channel_id=1, source_target_pairs={{1,0},{2,1},{3,2},{4,3},{5,4},{6,5},{7,6},{9,8},{10,9},{11,10},{12... | collective-permute-start | bytes 18440 | tf_op jit(solution)/shard_map/ppermute | solution.py:28
  12.0 47.2 %collective-permute-start.1 = (f32[3,16,1,128]{3,2,1,0:T(1,128)S(1)}, f32[3,16,1,128]{3,2,1,0:T(1,128)S(1)}, u32[]{:S(2)}, u32[]{:S(2)}) collective-permute-start(f32[3,16,1,128]{3,2,1,0:T(1,128)S(1)} %get-tuple-element.42), channel_id=1, source_target_pairs={{0,8},{8,16},{16,24},{1,9},{9,17},{17,25},{2,10},{10,18},{18,26},{... | collective-permute-start | bytes 73736 | tf_op jit(solution)/shard_map/ppermute | solution.py:27
  15.5 43.8 %collective-permute-start.4 = (f32[3,16,1,128]{3,2,1,0:T(1,128)S(1)}, f32[3,16,1,128]{3,2,1,0:T(1,128)S(1)}, u32[]{:S(2)}, u32[]{:S(2)}) collective-permute-start(f32[3,16,1,128]{3,2,1,0:T(1,128)S(1)} %get-tuple-element.43), channel_id=1, source_target_pairs={{8,0},{16,8},{24,16},{9,1},{17,9},{25,17},{10,2},{18,10},{26,18},{... | collective-permute-start | bytes 73736 | tf_op jit(solution)/shard_map/ppermute | solution.py:28
  57.0 3.3 %collective-permute-start.3 = (f32[3,1,32,128]{3,2,1,0:T(8,128)}, f32[3,1,32,128]{3,2,1,0:T(8,128)S(1)}, u32[]{:S(2)}, u32[]{:S(2)}) collective-permute-start(f32[3,1,32,128]{3,2,1,0:T(8,128)} %get-tuple-element.44), channel_id=1, source_target_pairs={{32,0},{64,32},{96,64},{128,96},{160,128},{192,160},{224,192},{33,... | collective-permute-start | bytes 147464 | tf_op jit(solution)/shard_map/ppermute | solution.py:28
  63.0 147.5 %copy-start = (f32[16,32,128]{2,1,0:T(8,128)}, f32[16,32,128]{2,1,0:T(8,128)S(1)}, u32[]{:S(2)}) copy-start(f32[16,32,128]{2,1,0:T(8,128)S(1)} %divide_minimum_fusion) | copy-start | bytes 786436
  63.2 14.5 %collective-permute-start.8 = (f32[16,1,128]{2,1,0:T(1,128)S(1)}, f32[16,1,128]{2,1,0:T(1,128)S(1)}, u32[]{:S(2)}, u32[]{:S(2)}) collective-permute-start(f32[16,1,128]{2,1,0:T(1,128)S(1)} %get-tuple-element.55), channel_id=1, source_target_pairs={{8,0},{16,8},{24,16},{9,1},{17,9},{25,17},{10,2},{18,10},{26,18},{... | collective-permute-start | bytes 24584 | tf_op jit(solution)/shard_map/ppermute | solution.py:28
  65.1 18.2 %collective-permute-start.10 = (f32[16,32,1]{2,1,0:T(8,128)S(1)}, f32[16,32,1]{2,1,0:T(8,128)S(1)}, u32[]{:S(2)}, u32[]{:S(2)}) collective-permute-start(f32[16,32,1]{2,1,0:T(8,128)S(1)} %get-tuple-element.53), channel_id=1, source_target_pairs={{1,0},{2,1},{3,2},{4,3},{5,4},{6,5},{7,6},{9,8},{10,9},{11,10},{12... | collective-permute-start | bytes 6152 | tf_op jit(solution)/shard_map/ppermute | solution.py:28
  66.4 16.9 %collective-permute-start.11 = (f32[16,32,1]{2,1,0:T(8,128)S(1)}, f32[16,32,1]{2,1,0:T(8,128)S(1)}, u32[]{:S(2)}, u32[]{:S(2)}) collective-permute-start(f32[16,32,1]{2,1,0:T(8,128)S(1)} %get-tuple-element.52), channel_id=1, source_target_pairs={{0,1},{1,2},{2,3},{3,4},{4,5},{5,6},{6,7},{8,9},{9,10},{10,11},{11... | collective-permute-start | bytes 6152 | tf_op jit(solution)/shard_map/ppermute | solution.py:27
  71.6 11.7 %collective-permute-start.6 = (f32[1,32,128]{2,1,0:T(8,128)S(1)}, f32[1,32,128]{2,1,0:T(8,128)S(1)}, u32[]{:S(2)}, u32[]{:S(2)}) collective-permute-start(f32[1,32,128]{2,1,0:T(8,128)S(1)} %get-tuple-element.57), channel_id=1, source_target_pairs={{32,0},{64,32},{96,64},{128,96},{160,128},{192,160},{224,192},{33,... | collective-permute-start | bytes 49160 | tf_op jit(solution)/shard_map/ppermute | solution.py:28
  72.9 10.4 %collective-permute-start.7 = (f32[1,32,128]{2,1,0:T(8,128)S(1)}, f32[1,32,128]{2,1,0:T(8,128)S(1)}, u32[]{:S(2)}, u32[]{:S(2)}) collective-permute-start(f32[1,32,128]{2,1,0:T(8,128)S(1)} %get-tuple-element.56), channel_id=1, source_target_pairs={{0,32},{32,64},{64,96},{96,128},{128,160},{160,192},{192,224},{1,3... | collective-permute-start | bytes 49160 | tf_op jit(solution)/shard_map/ppermute | solution.py:27
  77.7 5.5 %collective-permute-start.9 = (f32[16,1,128]{2,1,0:T(1,128)S(1)}, f32[16,1,128]{2,1,0:T(1,128)S(1)}, u32[]{:S(2)}, u32[]{:S(2)}) collective-permute-start(f32[16,1,128]{2,1,0:T(1,128)S(1)} %get-tuple-element.54), channel_id=1, source_target_pairs={{0,8},{8,16},{16,24},{1,9},{9,17},{17,25},{2,10},{10,18},{18,26},{... | collective-permute-start | bytes 24584 | tf_op jit(solution)/shard_map/ppermute | solution.py:27
  89.0 13.9 %collective-permute-start.16 = (f32[3,16,32,1]{2,1,3,0:T(8,128)S(1)}, f32[3,16,32,1]{2,1,3,0:T(8,128)S(1)}, u32[]{:S(2)}, u32[]{:S(2)}) collective-permute-start(f32[3,16,32,1]{2,1,3,0:T(8,128)S(1)} %copy.16), channel_id=1, source_target_pairs={{1,0},{2,1},{3,2},{4,3},{5,4},{6,5},{7,6},{9,8},{10,9},{11,10},{12... | collective-permute-start | bytes 18440 | tf_op jit(solution)/shard_map/ppermute | solution.py:28
  91.4 16.6 %collective-permute-start.17 = (f32[3,16,32,1]{2,1,3,0:T(8,128)S(1)}, f32[3,16,32,1]{2,1,3,0:T(8,128)S(1)}, u32[]{:S(2)}, u32[]{:S(2)}) collective-permute-start(f32[3,16,32,1]{2,1,3,0:T(8,128)S(1)} %copy.18), channel_id=1, source_target_pairs={{0,1},{1,2},{2,3},{3,4},{4,5},{5,6},{6,7},{8,9},{9,10},{10,11},{11... | collective-permute-start | bytes 18440 | tf_op jit(solution)/shard_map/ppermute | solution.py:27
  96.0 13.4 %collective-permute-start.12 = (f32[3,1,32,128]{3,2,1,0:T(8,128)}, f32[3,1,32,128]{3,2,1,0:T(8,128)S(1)}, u32[]{:S(2)}, u32[]{:S(2)}) collective-permute-start(f32[3,1,32,128]{3,2,1,0:T(8,128)} %get-tuple-element.37), channel_id=1, source_target_pairs={{32,0},{64,32},{96,64},{128,96},{160,128},{192,160},{224,192},{33,... | collective-permute-start | bytes 147464 | tf_op jit(solution)/shard_map/ppermute | solution.py:28
  97.3 12.1 %collective-permute-start.13 = (f32[3,1,32,128]{3,2,1,0:T(8,128)}, f32[3,1,32,128]{3,2,1,0:T(8,128)}, u32[]{:S(2)}, u32[]{:S(2)}) collective-permute-start(f32[3,1,32,128]{3,2,1,0:T(8,128)} %get-tuple-element.36), channel_id=1, source_target_pairs={{0,32},{32,64},{64,96},{96,128},{128,160},{160,192},{192,224},{1,3... | collective-permute-start | bytes 147464 | tf_op jit(solution)/shard_map/ppermute | solution.py:27
  101.0 8.4 %collective-permute-start.14 = (f32[3,16,1,128]{3,2,1,0:T(1,128)}, f32[3,16,1,128]{3,2,1,0:T(1,128)S(1)}, u32[]{:S(2)}, u32[]{:S(2)}) collective-permute-start(f32[3,16,1,128]{3,2,1,0:T(1,128)} %get-tuple-element.39), channel_id=1, source_target_pairs={{8,0},{16,8},{24,16},{9,1},{17,9},{25,17},{10,2},{18,10},{26,18},{... | collective-permute-start | bytes 73736 | tf_op jit(solution)/shard_map/ppermute | solution.py:28
  102.9 6.5 %collective-permute-start.15 = (f32[3,16,1,128]{3,2,1,0:T(1,128)}, f32[3,16,1,128]{3,2,1,0:T(1,128)S(1)}, u32[]{:S(2)}, u32[]{:S(2)}) collective-permute-start(f32[3,16,1,128]{3,2,1,0:T(1,128)} %get-tuple-element.38), channel_id=1, source_target_pairs={{0,8},{8,16},{16,24},{1,9},{9,17},{17,25},{2,10},{10,18},{18,26},{... | collective-permute-start | bytes 73736 | tf_op jit(solution)/shard_map/ppermute | solution.py:27
  112.6 31.5 %copy-start.1 = (f32[3,16,32,128]{3,2,1,0:T(8,128)}, f32[3,16,32,128]{3,2,1,0:T(8,128)S(1)}, u32[]{:S(2)}) copy-start(f32[3,16,32,128]{3,2,1,0:T(8,128)S(1)} %fusion.22) | copy-start | bytes 2359300
  115.4 15.9 %collective-permute-start.28 = (f32[3,16,32,1]{2,1,3,0:T(8,128)}, f32[3,16,32,1]{2,1,3,0:T(8,128)S(1)}, u32[]{:S(2)}, u32[]{:S(2)}) collective-permute-start(f32[3,16,32,1]{2,1,3,0:T(8,128)} %copy.24), channel_id=1, source_target_pairs={{1,0},{2,1},{3,2},{4,3},{5,4},{6,5},{7,6},{9,8},{10,9},{11,10},{12... | collective-permute-start | bytes 18440 | tf_op jit(solution)/shard_map/ppermute | solution.py:28
  118.9 18.3 %collective-permute-start.29 = (f32[3,16,32,1]{2,1,3,0:T(8,128)S(1)}, f32[3,16,32,1]{2,1,3,0:T(8,128)S(1)}, u32[]{:S(2)}, u32[]{:S(2)}) collective-permute-start(f32[3,16,32,1]{2,1,3,0:T(8,128)S(1)} %copy.26), channel_id=1, source_target_pairs={{0,1},{1,2},{2,3},{3,4},{4,5},{5,6},{6,7},{8,9},{9,10},{10,11},{11... | collective-permute-start | bytes 18440 | tf_op jit(solution)/shard_map/ppermute | solution.py:27
  124.5 19.6 %collective-permute-start.24 = (f32[3,1,32,128]{3,2,1,0:T(8,128)}, f32[3,1,32,128]{3,2,1,0:T(8,128)S(1)}, u32[]{:S(2)}, u32[]{:S(2)}) collective-permute-start(f32[3,1,32,128]{3,2,1,0:T(8,128)} %get-tuple-element.33), channel_id=1, source_target_pairs={{32,0},{64,32},{96,64},{128,96},{160,128},{192,160},{224,192},{33,... | collective-permute-start | bytes 147464 | tf_op jit(solution)/shard_map/ppermute | solution.py:28
  125.8 18.3 %collective-permute-start.25 = (f32[3,1,32,128]{3,2,1,0:T(8,128)}, f32[3,1,32,128]{3,2,1,0:T(8,128)}, u32[]{:S(2)}, u32[]{:S(2)}) collective-permute-start(f32[3,1,32,128]{3,2,1,0:T(8,128)} %get-tuple-element.32), channel_id=1, source_target_pairs={{0,32},{32,64},{64,96},{96,128},{128,160},{160,192},{192,224},{1,3... | collective-permute-start | bytes 147464 | tf_op jit(solution)/shard_map/ppermute | solution.py:27
  129.4 11.8 %collective-permute-start.26 = (f32[3,16,1,128]{3,2,1,0:T(1,128)}, f32[3,16,1,128]{3,2,1,0:T(1,128)}, u32[]{:S(2)}, u32[]{:S(2)}) collective-permute-start(f32[3,16,1,128]{3,2,1,0:T(1,128)} %get-tuple-element.31), channel_id=1, source_target_pairs={{8,0},{16,8},{24,16},{9,1},{17,9},{25,17},{10,2},{18,10},{26,18},{... | collective-permute-start | bytes 73736 | tf_op jit(solution)/shard_map/ppermute | solution.py:28
  131.3 11.9 %collective-permute-start.27 = (f32[3,16,1,128]{3,2,1,0:T(1,128)}, f32[3,16,1,128]{3,2,1,0:T(1,128)}, u32[]{:S(2)}, u32[]{:S(2)}) collective-permute-start(f32[3,16,1,128]{3,2,1,0:T(1,128)} %get-tuple-element.30), channel_id=1, source_target_pairs={{0,8},{8,16},{16,24},{1,9},{9,17},{17,25},{2,10},{10,18},{18,26},{... | collective-permute-start | bytes 73736 | tf_op jit(solution)/shard_map/ppermute | solution.py:27
  137.2 23.0 %collective-permute-start.18 = (f32[7,32,128]{2,1,0:T(8,128)}, f32[7,32,128]{2,1,0:T(8,128)}, u32[]{:S(2)}, u32[]{:S(2)}) collective-permute-start(f32[7,32,128]{2,1,0:T(8,128)} %get-tuple-element.50), channel_id=1, source_target_pairs={{0,32},{32,64},{64,96},{96,128},{128,160},{160,192},{192,224},{1,3... | collective-permute-start | bytes 344072 | tf_op jit(solution)/shard_map/ppermute | solution.py:48
  141.2 19.0 %collective-permute-start.19 = (f32[7,32,128]{2,1,0:T(8,128)}, f32[7,32,128]{2,1,0:T(8,128)}, u32[]{:S(2)}, u32[]{:S(2)}) collective-permute-start(f32[7,32,128]{2,1,0:T(8,128)} %get-tuple-element.51), channel_id=1, source_target_pairs={{32,0},{64,32},{96,64},{128,96},{160,128},{192,160},{224,192},{33,... | collective-permute-start | bytes 344072 | tf_op jit(solution)/shard_map/ppermute | solution.py:51
  161.1 19.0 %collective-permute-start.20 = (f32[30,7,128]{2,1,0:T(8,128)S(1)}, f32[30,7,128]{2,1,0:T(8,128)S(1)}, u32[]{:S(2)}, u32[]{:S(2)}) collective-permute-start(f32[30,7,128]{2,1,0:T(8,128)S(1)} %get-tuple-element.48), channel_id=1, source_target_pairs={{0,8},{8,16},{16,24},{1,9},{9,17},{17,25},{2,10},{10,18},{18,26},{... | collective-permute-start | bytes 322568 | tf_op jit(solution)/shard_map/ppermute | solution.py:48
  165.3 14.8 %collective-permute-start.21 = (f32[30,7,128]{2,1,0:T(8,128)S(1)}, f32[30,7,128]{2,1,0:T(8,128)S(1)}, u32[]{:S(2)}, u32[]{:S(2)}) collective-permute-start(f32[30,7,128]{2,1,0:T(8,128)S(1)} %get-tuple-element.49), channel_id=1, source_target_pairs={{8,0},{16,8},{24,16},{9,1},{17,9},{25,17},{10,2},{18,10},{26,18},{... | collective-permute-start | bytes 322568 | tf_op jit(solution)/shard_map/ppermute | solution.py:51
  181.8 27.9 %collective-permute-start.22 = (f32[30,46,7]{1,0,2:T(8,128)S(1)}, f32[30,46,7]{1,0,2:T(8,128)S(1)}, u32[]{:S(2)}, u32[]{:S(2)}) collective-permute-start(f32[30,46,7]{1,0,2:T(8,128)S(1)} %copy.20), channel_id=1, source_target_pairs={{0,1},{1,2},{2,3},{3,4},{4,5},{5,6},{6,7},{8,9},{9,10},{10,11},{11... | collective-permute-start | bytes 115928 | tf_op jit(solution)/shard_map/ppermute | solution.py:48
  187.0 23.1 %collective-permute-start.23 = (f32[30,46,7]{1,0,2:T(8,128)S(1)}, f32[30,46,7]{1,0,2:T(8,128)S(1)}, u32[]{:S(2)}, u32[]{:S(2)}) collective-permute-start(f32[30,46,7]{1,0,2:T(8,128)S(1)} %copy.21), channel_id=1, source_target_pairs={{1,0},{2,1},{3,2},{4,3},{5,4},{6,5},{7,6},{9,8},{10,9},{11,10},{12... | collective-permute-start | bytes 115928 | tf_op jit(solution)/shard_map/ppermute | solution.py:51
  (22 other events, 255.3 us)
where the time goes:
time: 234 us; the launch traced here: 233 us
  starting transfers between devices  83.6 us (36%)
  local copies, waits for them, and re-layouts  67.2 us (29%)
  blocking collectives  45.3 us (19%)
  other arithmetic  32.1 us (14%)
  between operations  3.51 us (2%)
    ppermute x12, starting transfers between devices, padded_2(): lax.ppermute(last, axis, up)  48.7 us
    psum x4, blocking collectives, by_axis(): return functools.reduce(lax.psum, axes, shard)  45.3 us
    ppermute x12, starting transfers between devices, padded_2(): lax.ppermute(initial, axis, [(b, a) for a, b in up])  18.5 us
    slice x24, local copies, waits for them, and re-layouts, every_other(): lax.slice_in_dim(field, start, start + 2 * coarse_len - 1, 2, dim_index)  16.7 us
    reshape x2, local copies, waits for them, and re-layouts, expand_table(): return spread.reshape(blocks_x * BLOCK, blocks_y * BLOCK, blocks_z * BLOCK)  16.3 us
    ppermute x3, starting transfers between devices, padded_3(): lax.ppermute(lax.slice_in_dim(block, block.shape[dim] - width, None, axis...  11.8 us
    add x2, other arithmetic, expand_table(): block_table + jnp.where(phase_block == phase_id, table[phase_id], 0.0)  10 us
    broadcast_in_dim x2, local copies, waits for them, and re-layouts, expand_table(): jnp.broadcast_to(block_table[:, None, :, None, :, None], (blocks_x, BLOCK...  8.89 us
  transfers between devices with their start and end apart: 30, of which 2 were waited for; matrix products, arithmetic and copies ran while one was open for 26% of the time, Pallas kernels for 0%

commit v1 on v0

v1 whole, which is shorter than its diff:
```python
import functools

import jax
import jax.numpy as jnp
import numpy as np
from jax import lax
from jax.experimental import pallas as pl
from jax.experimental.pallas import tpu as pltpu
from jax.sharding import PartitionSpec as P

MESH = pl.DeviceIdType.MESH
RELAX = 0.8
F32 = jnp.float32
G = 4

ROWS = (128, 32, 8)
LANES = ((0, 64), (64, 32), (96, 16))


def depth_operator():
    out = np.zeros((4, 136, 128), np.float32)
    for low_edge in range(2):
        for high_edge in range(2):
            ext = np.eye(128, dtype=np.float64)
            n = 128
            table = out[low_edge * 2 + high_edge]
            first = 0
            for level, (lane, own) in enumerate(LANES):
                n //= 2
                new = np.zeros((n + 2, 128))
                for k in range(-1, n + 1):
                    for offset, weight in ((-1, 1), (0, 3), (1, 3), (2, 1)):
                        i = 2 * k + offset + first
                        if 0 <= i < ext.shape[0]:
                            new[k + 1] += weight / 8 * ext[i]
                if low_edge:
                    new[0] = 0
                if high_edge:
                    new[-1] = 0
                ext, first = new, 1
                table[:128, lane : lane + own] = new[1:-1].T
                table[128 + 2 * level] = new[0]
                table[129 + 2 * level] = new[-1]
    return out


def depth_places():
    sel = np.zeros((16, 128), np.float32)
    for level, (lane, own) in enumerate(LANES):
        sel[1 + 2 * level, lane] = 1
        sel[8 + 2 * level, lane + own - 1] = 1
    return sel


def kernel(
    sizes,
    u_hbm, f_hbm, phase_ref, op_hbm, sel_ref, pref_ref, yield_ref,
    smooth_hbm, visc_hbm, c1_ref, c2_ref, c3_ref, resid_hbm, rms_ref,
    u0, u1, u2, frc, vis, fx, fy, fzl, fzh, rdiag, res,
    cells, yr, ys, zr, zs, vyr, vys, vzr, vzs,
    ap, t1, t2, t3, cxs, cxr, cys, cyr, czs, czr, bc, opm,
    ar_a, ar_b,
    load_sem, out_sem, snd, rcv, vsnd, vrcv, csnd, crcv, asnd, arcv,
):
    nx, ny, nz = sizes
    gx, gy, gz = lax.axis_index("gx"), lax.axis_index("gy"), lax.axis_index("gz")
    coords = {"gx": gx, "gy": gy, "gz": gz}
    has = {
        "gx": (gx > 0, gx < nx - 1),
        "gy": (gy > 0, gy < ny - 1),
        "gz": (gz > 0, gz < nz - 1),
    }
    axes = ("gx", "gy", "gz")

    load_u = pltpu.make_async_copy(u_hbm, u0.at[:, 1:17, 8:40, :], load_sem.at[0])
    load_f = pltpu.make_async_copy(f_hbm, frc, load_sem.at[1])
    edge = (gz == 0).astype(jnp.int32) * 2 + (gz == nz - 1).astype(jnp.int32)
    load_op = pltpu.make_async_copy(op_hbm.at[edge], opm, load_sem.at[2])
    load_u.start()
    load_f.start()
    load_op.start()

    barrier = pltpu.get_barrier_semaphore()

    def greet(i, carry):
        @pl.when(i != gz)
        def _():
            pl.semaphore_signal(barrier, inc=1, device_id={"gz": i}, device_id_type=MESH)
        return carry

    def greet_plane(i, carry):
        px, py = i // ny, i % ny

        @pl.when((px != gx) | (py != gy))
        def _():
            pl.semaphore_signal(barrier, inc=1, device_id={"gx": px, "gy": py}, device_id_type=MESH)
        return carry

    lax.fori_loop(0, nz, greet, 0)
    lax.fori_loop(0, nx * ny, greet_plane, 0)

    lane = lax.broadcasted_iota(jnp.int32, (8, 128), 1)
    lane32 = lax.broadcasted_iota(jnp.int32, (32, 128), 1)

    @pl.when(gx == 0)
    def _():
        zero = jnp.zeros((3, 32, 128), F32)
        for u in (u0, u1, u2):
            u[:, 0, 8:40, :] = zero
        vis[0, 8:40, :] = jnp.zeros((32, 128), F32)
        cxr[0] = jnp.zeros((48, 128), F32)

    @pl.when(gx == nx - 1)
    def _():
        zero = jnp.zeros((3, 32, 128), F32)
        for u in (u0, u1, u2):
            u[:, 17, 8:40, :] = zero
        vis[17, 8:40, :] = jnp.zeros((32, 128), F32)
        cxr[1] = jnp.zeros((48, 128), F32)

    for side, there in enumerate((gy == 0, gy == ny - 1)):
        @pl.when(there)
        def _(side=side):
            for phase in range(3):
                yr[phase, side] = jnp.zeros((3, 16, 128), F32)
            vyr[side] = jnp.zeros((16, 128), F32)
            cyr[side] = jnp.zeros((24, 128), F32)

    for side, there in enumerate((gz == 0, gz == nz - 1)):
        @pl.when(there)
        def _(side=side):
            for phase in range(3):
                zr[phase, side] = jnp.zeros((3, 8, 128), F32)
            vzr[side] = jnp.zeros((8, 128), F32)
            czr[side] = jnp.zeros((8, 256), F32)

    ap[:, 0:8, :] = jnp.zeros((20, 8, 128), F32)
    ap[:, 40:48, :] = jnp.zeros((20, 8, 128), F32)
    t1[...] = jnp.zeros(t1.shape, F32)
    t2[...] = jnp.zeros(t2.shape, F32)

    blocks = phase_ref[...].reshape(32, 32)
    row = lax.broadcasted_iota(jnp.int32, (32, 128), 0)
    spread_z = (lane32 // 4 == row).astype(F32)
    r = lax.broadcasted_iota(jnp.int32, (128, 32), 0)
    c = lax.broadcasted_iota(jnp.int32, (128, 32), 1)
    spread_y = ((r // 32) * 8 + (r % 32) // 4 == c).astype(F32)
    for which, table in enumerate((pref_ref, yield_ref)):
        values = jnp.zeros((32, 32), F32)
        for phase in range(8):
            values = jnp.where(blocks == phase, table[phase], values)
        wide = jnp.dot(values, spread_z, precision=lax.Precision.HIGHEST, preferred_element_type=F32)
        cells[which] = jnp.dot(spread_y, wide, precision=lax.Precision.HIGHEST, preferred_element_type=F32)

    def copies(axis, lo_src, lo_dst, hi_src, hi_dst, send, recv):
        k = axes.index(axis)
        lo = pltpu.make_async_remote_copy(
            lo_src, lo_dst, send.at[k, 0], recv.at[k, 1],
            device_id={axis: coords[axis] - 1}, device_id_type=MESH)
        hi = pltpu.make_async_remote_copy(
            hi_src, hi_dst, send.at[k, 1], recv.at[k, 0],
            device_id={axis: coords[axis] + 1}, device_id_type=MESH)
        return axis, lo, hi

    def start(pair):
        axis, lo, hi = pair

        @pl.when(has[axis][0])
        def _():
            lo.start()

        @pl.when(has[axis][1])
        def _():
            hi.start()

    def wait(pair):
        axis, lo, hi = pair

        @pl.when(has[axis][0])
        def _():
            lo.wait_send()
            hi.wait_recv()

        @pl.when(has[axis][1])
        def _():
            hi.wait_send()
            lo.wait_recv()

    def field_copies(phase, u):
        s, w = snd.at[phase], rcv.at[phase]
        return (
            copies("gz", zs.at[phase], zr.at[phase, 1], zs.at[phase], zr.at[phase, 0], s, w),
            copies("gx", u.at[:, 1, 8:40, :], u.at[:, 17, 8:40, :], u.at[:, 16, 8:40, :], u.at[:, 0, 8:40, :], s, w),
            copies("gy", ys.at[phase, 0], yr.at[phase, 1], ys.at[phase, 1], yr.at[phase, 0], s, w),
        )

    def take_rows(phase, u):
        for comp in range(3):
            for x in range(16):
                u[comp, x + 1, 7:8, :] = yr[phase, 0, comp, x : x + 1, :]
                u[comp, x + 1, 40:41, :] = yr[phase, 1, comp, x : x + 1, :]

    def merged(low, high):
        return jnp.where(lane % 2 == 0, pltpu.roll(high, 127, 1), pltpu.roll(low, 1, 1))

    def ends_of(column, x):
        return jnp.concatenate([pltpu.roll(column, 127 - 8 * x - 2 * t, 1) for t in range(4)], axis=0)

    def packed(acc, plane, x):
        for t in range(4):
            i = 4 * x + t
            acc = jnp.where(lane // 2 == i, pltpu.roll(plane[8 * t : 8 * t + 8], 2 * i + 1, 1), acc)
        return acc

    def along_z(centre, ends):
        up = jnp.where(lane32 == 127, ends, pltpu.roll(centre, 127, 1))
        down = jnp.where(lane32 == 0, ends, pltpu.roll(centre, 1, 1))
        return up, down

    def planes(body, carry):
        def step(i, carry):
            for j in range(G):
                carry = body(i * G + j, carry)
            return carry
        return lax.fori_loop(0, 16 // G, step, carry)

    def pack_rows(phase, comp, x, plane):
        ys[phase, 0, comp, pl.ds(x, 1), :] = plane[0:1]
        ys[phase, 1, comp, pl.ds(x, 1), :] = plane[31:32]

    zero3 = (jnp.zeros((8, 128), F32),) * 3

    load_u.wait()

    def pack_body(x, acc):
        acc = list(acc)
        for comp in range(3):
            plane = u0[comp, x + 1, 8:40, :]
            pack_rows(0, comp, x, plane)
            acc[comp] = packed(acc[comp], plane, x)
        return tuple(acc)

    acc = planes(pack_body, zero3)
    for comp in range(3):
        zs[0, comp] = acc[comp]
    pl.semaphore_wait(barrier, (nz - 1) + (nx * ny - 1))
    sent = field_copies(0, u0)
    for pair in sent:
        start(pair)
    for pair in sent:
        wait(pair)
    take_rows(0, u0)

    def visc_body(x, acc):
        d = []
        for comp in range(3):
            centre = u0[comp, x + 1, 8:40, :]
            up, down = along_z(centre, ends_of(ends[comp], x))
            d.append((
                u0[comp, x + 2, 8:40, :] - u0[comp, x, 8:40, :],
                u0[comp, x + 1, 9:41, :] - u0[comp, x + 1, 7:39, :],
                up - down,
            ))
        diag = d[0][0] * d[0][0] + d[1][1] * d[1][1] + d[2][2] * d[2][2]
        xy, xz, yz = d[0][1] + d[1][0], d[0][2] + d[2][0], d[1][2] + d[2][1]
        off = xy * xy + xz * xz + yz * yz
        inv = diag * 0.125 + off * 0.0625 + 1.0
        block = pl.ds(pl.multiple_of((x // 4) * 32, 32), 32)
        creep = cells[0, block, :] * jnp.exp(jnp.log(inv) * (-1.0 / 3.0))
        plastic = cells[1, block, :] * (0.5 * lax.rsqrt(inv))
        v = jnp.minimum(creep, plastic)
        vis[x + 1, 8:40, :] = v
        vys[0, pl.ds(x, 1), :] = v[0:1]
        vys[1, pl.ds(x, 1), :] = v[31:32]
        return packed(acc, v, x)

    ends = [merged(zr[0, 0, comp], zr[0, 1, comp]) for comp in range(3)]
    vzs[...] = planes(visc_body, jnp.zeros((8, 128), F32))
    vsent = (
        copies("gz", vzs, vzr.at[1], vzs, vzr.at[0], vsnd, vrcv),
        copies("gx", vis.at[1, 8:40, :], vis.at[17, 8:40, :], vis.at[16, 8:40, :], vis.at[0, 8:40, :], vsnd, vrcv),
        copies("gy", vys.at[0], vyr.at[1], vys.at[1], vyr.at[0], vsnd, vrcv),
    )
    for pair in vsent:
        start(pair)
    put_visc = pltpu.make_async_copy(vis.at[1:17, 8:40, :], visc_hbm, out_sem.at[0])
    put_visc.start()

    flag = {a: tuple(jnp.where(h, 1.0, 0.0).astype(F32) for h in has[a]) for a in axes}

    def weighted(get, k, count):
        total = None
        for offset, weight in ((-1, 0.125), (0, 0.375), (1, 0.375), (2, 0.125)):
            i = 2 * k + offset
            if 0 <= i < count:
                term = get(i) * weight
                total = term if total is None else total + term
        return total

    first = 0
    count = 16
    base = 0
    prev = None
    for level, own in enumerate((8, 4, 2)):
        for k in range(-1, own + 1):
            if level == 0:
                value = weighted(lambda i: vis[i + 1, 8:40, :], k, 16)
            else:
                value = None
                for offset, weight in ((-1, 0.125), (0, 0.375), (1, 0.375), (2, 0.125)):
                    i = 2 * k + offset + 1
                    if 0 <= i < prev[1]:
                        term = ap[prev[0] + i, 8:40, :] * weight
                        value = term if value is None else value + term
            if k == -1:
                value = value * flag["gx"][0]
            if k == own:
                value = value * flag["gx"][1]
            ap[base + k + 1, 8:40, :] = value
        prev = (base, own + 2)
        base += own + 2

    def halve(src, start, rows):
        return (
            (src[:, pl.ds(5, rows, stride=2), :] + src[:, pl.ds(8, rows, stride=2), :])
            + 3.0 * (src[:, pl.ds(6, rows, stride=2), :] + src[:, pl.ds(7, rows, stride=2), :])
        ) * 0.125

    low_y, high_y = flag["gy"]
    t1[:, 7:25, :] = halve(ap, 5, 18)
    t1[:, 7:8, :] = t1[:, 7:8, :] * low_y
    t1[:, 24:25, :] = t1[:, 24:25, :] * high_y
    t2[:, 7:17, :] = halve(t1.at[10:20], 5, 10)
    t2[:, 7:8, :] = t2[:, 7:8, :] * low_y
    t2[:, 16:17, :] = t2[:, 16:17, :] * high_y
    t3[:, 7:13, :] = halve(t2.at[6:10], 5, 6)
    t3[:, 7:8, :] = t3[:, 7:8, :] * low_y
    t3[:, 12:13, :] = t3[:, 12:13, :] * high_y

    levels = ((t1, 0, 8, 16, 0, 0), (t2, 0, 4, 8, 24, 8), (t3, 0, 2, 4, 40, 16))
    for t, _, own, rows, at, _ in levels:
        cxs[0, at : at + rows + 2, :] = t[0, 7 : rows + 9, :]
        cxs[1, at : at + rows + 2, :] = t[own + 1, 7 : rows + 9, :]
    cx = copies("gx", cxs.at[0], cxr.at[1], cxs.at[1], cxr.at[0], csnd, crcv)
    start(cx)

    for pair in vsent:
        wait(pair)
    for x in range(16):
        vis[x + 1, 7:8, :] = vyr[0, x : x + 1, :]
        vis[x + 1, 40:41, :] = vyr[1, x : x + 1, :]
    load_f.wait()
    vends = merged(vzr[0], vzr[1])

    def sums(u, column, x, faces):
        centre = u[x + 1, 8:40, :]
        up, down = along_z(centre, ends_of(column, x))
        total = faces[0] * u[x, 8:40, :] + faces[1] * u[x + 2, 8:40, :]
        total = total + (faces[2] * u[x + 1, 7:39, :] + faces[3] * u[x + 1, 9:41, :])
        return centre, total + (faces[4] * down + faces[5] * up)

    def first_body(x, acc):
        centre = vis[x + 1, 8:40, :]
        up, down = along_z(centre, ends_of(vends, x))
        half = 0.5 * centre
        faces = [
            half + 0.5 * vis[x, 8:40, :],
            half + 0.5 * vis[x + 2, 8:40, :],
            half + 0.5 * vis[x + 1, 7:39, :],
            half + 0.5 * vis[x + 1, 9:41, :],
            half + 0.5 * down,
            half + 0.5 * up,
        ]
        fx[x] = faces[0]
        fx[x + 1] = faces[1]
        fy[0, x] = faces[2]
        fy[1, x] = faces[3]
        fzl[x] = faces[4]
        fzh[x] = faces[5]
        diag = ((faces[0] + faces[1]) + (faces[2] + faces[3])) + (faces[4] + faces[5])
        scale = RELAX / diag
        rdiag[0, x] = scale
        rdiag[1, x] = diag
        acc = list(acc)
        for comp in range(3):
            centre, total = sums(u0.at[comp], ends[comp], x, faces)
            new = (1.0 - RELAX) * centre + scale * (frc[comp, x] + total)
            u1[comp, x + 1, 8:40, :] = new
            pack_rows(1, comp, x, new)
            acc[comp] = packed(acc[comp], new, x)
        return tuple(acc)

    def faces_of(x):
        return [fx[x], fx[x + 1], fy[0, x], fy[1, x], fzl[x], fzh[x]]

    acc = planes(first_body, zero3)
    for comp in range(3):
        zs[1, comp] = acc[comp]
    sent = field_copies(1, u1)
    for pair in sent:
        start(pair)

    wait(cx)
    for t, _, own, rows, at, _ in levels:
        t[1, 7 : rows + 9, :] = t[1, 7 : rows + 9, :] + cxr[0, at : at + rows + 2, :]
        t[own, 7 : rows + 9, :] = t[own, 7 : rows + 9, :] + cxr[1, at : at + rows + 2, :]
    for t, _, own, rows, _, at in levels:
        for k in range(own):
            cys[0, at + k : at + k + 1, :] = t[k + 1, 7:8, :]
            cys[1, at + k : at + k + 1, :] = t[k + 1, rows + 8 : rows + 9, :]
    cy = copies("gy", cys.at[0], cyr.at[1], cys.at[1], cyr.at[0], csnd, crcv)
    start(cy)

    for pair in sent:
        wait(pair)
    take_rows(1, u1)
    ends = [merged(zr[1, 0, comp], zr[1, 1, comp]) for comp in range(3)]

    def second_body(x, acc):
        faces = faces_of(x)
        scale = rdiag[0, x]
        acc = list(acc)
        for comp in range(3):
            centre, total = sums(u1.at[comp], ends[comp], x, faces)
            new = (1.0 - RELAX) * centre + scale * (frc[comp, x] + total)
            u2[comp, x + 1, 8:40, :] = new
            pack_rows(2, comp, x, new)
            acc[comp] = packed(acc[comp], new, x)
        return tuple(acc)

    acc = planes(second_body, zero3)
    for comp in range(3):
        zs[2, comp] = acc[comp]
    sent = field_copies(2, u2)
    for pair in sent:
        start(pair)
    put_smooth = pltpu.make_async_copy(u2.at[:, 1:17, 8:40, :], smooth_hbm, out_sem.at[1])
    put_smooth.start()

    wait(cy)
    at = 0
    for t, _, own, rows, _, place in levels:
        for k in range(own):
            value = t[k + 1, 8 : rows + 8, :]
            r = lax.broadcasted_iota(jnp.int32, (rows, 128), 0)
            value = value + jnp.where(r == 0, cyr[0, place + k : place + k + 1, :], 0.0)
            value = value + jnp.where(r == rows - 1, cyr[1, place + k : place + k + 1, :], 0.0)
            bc[at : at + rows, :] = value
            at += rows
    load_op.wait()
    czs[...] = jnp.zeros((8, 256), F32)
    czs[:, 0:168] = lax.dot_general(
        opm[128:136, :], bc[...], (((1,), (1,)), ((), ())),
        precision=lax.Precision.HIGHEST, preferred_element_type=F32)
    cz = copies("gz", czs, czr.at[1], czs, czr.at[0], csnd, crcv)
    start(cz)

    for pair in sent:
        wait(pair)
    take_rows(2, u2)
    ends = [merged(zr[2, 0, comp], zr[2, 1, comp]) for comp in range(3)]

    def resid_body(x, acc):
        faces = faces_of(x)
        diag = rdiag[1, x]
        for comp in range(3):
            centre, total = sums(u2.at[comp], ends[comp], x, faces)
            left = frc[comp, x] + total - diag * centre
            res[comp, x] = left
            square = left * left
            acc = acc + ((square[0:8] + square[8:16]) + (square[16:24] + square[24:32]))
        return acc

    acc = planes(resid_body, jnp.zeros((8, 128), F32))

    ar_a[gz] = jnp.sum(acc, axis=0, keepdims=True)

    def row_copy(i):
        return pltpu.make_async_remote_copy(
            ar_a.at[gz], ar_a.at[gz], asnd.at[0], arcv.at[0], device_id={"gz": i}, device_id_type=MESH)

    def send_row(i, carry):
        @pl.when(i != gz)
        def _():
            row_copy(i).start()
        return carry

    lax.fori_loop(0, nz, send_row, 0)
    put_res = pltpu.make_async_copy(res, resid_hbm, out_sem.at[2])
    put_res.start()

    wait(cz)
    got = jnp.concatenate([czr[0], czr[1]], axis=0)[:, 0:168]
    coarse = jnp.dot(bc[...], opm[0:128, :], precision=lax.Precision.HIGHEST, preferred_element_type=F32)
    coarse = coarse + lax.dot_general(
        got, sel_ref[...], (((0,), (0,)), ((), ())),
        precision=lax.Precision.HIGHEST, preferred_element_type=F32)
    c1_ref[...] = coarse[0:128, 0:64].reshape(8, 16, 64)
    c2_ref[...] = coarse[128:160, 64:96].reshape(4, 8, 32)
    c3_ref[0] = coarse[160:164, 96:112]
    c3_ref[1] = coarse[164:168, 96:112]

    def whole(buf, n, sem):
        return pltpu.make_async_copy(buf.at[0:n], buf.at[0:n], sem)

    whole(ar_a, nz - 1, asnd.at[0]).wait()
    whole(ar_a, nz - 1, arcv.at[0]).wait()
    mine = gx * ny + gy
    line = ar_a[0]
    for i in range(1, nz):
        line = line + ar_a[i]
    ar_b[mine] = line

    def send_plane(i, carry):
        px, py = i // ny, i % ny

        @pl.when((px != gx) | (py != gy))
        def _():
            pltpu.make_async_remote_copy(
                ar_b.at[mine], ar_b.at[mine], asnd.at[1], arcv.at[1],
                device_id={"gx": px, "gy": py}, device_id_type=MESH).start()
        return carry

    lax.fori_loop(0, nx * ny, send_plane, 0)
    put_visc.wait()
    put_smooth.wait()
    put_res.wait()
    whole(ar_b, nx * ny - 1, asnd.at[1]).wait()
    whole(ar_b, nx * ny - 1, arcv.at[1]).wait()
    total = jnp.sum(ar_b[...], axis=0)
    cells_all = float(3 * 16 * nx * 32 * ny * 128 * nz)
    rms_ref[...] = jnp.sqrt(jnp.sum(total, axis=1, keepdims=True) / cells_all)


def per_device(sizes, velocity, forcing, phase_block, prefactor, yield_stress):
    nx, ny, nz = sizes
    vm = lambda *shape: pltpu.VMEM(shape, F32)
    any_, vmem, smem = (pl.BlockSpec(memory_space=s) for s in (pl.ANY, pltpu.VMEM, pltpu.SMEM))
    shape = lambda *s: jax.ShapeDtypeStruct(s, F32)
    out = pl.pallas_call(
        functools.partial(kernel, sizes),
        out_shape=(
            shape(3, 16, 32, 128), shape(16, 32, 128), shape(8, 16, 64), shape(4, 8, 32), shape(2, 4, 16),
            shape(3, 16, 32, 128), shape(1, 1),
        ),
        in_specs=[any_, any_, vmem, any_, vmem, smem, smem],
        out_specs=(any_, any_, vmem, vmem, vmem, any_, vmem),
        scratch_shapes=[
            vm(3, 18, 48, 128), vm(3, 18, 48, 128), vm(3, 18, 48, 128), vm(3, 16, 32, 128), vm(18, 48, 128),
            vm(17, 32, 128), vm(2, 16, 32, 128), vm(16, 32, 128), vm(16, 32, 128), vm(2, 16, 32, 128), vm(3, 16, 32, 128),
            vm(2, 128, 128), vm(3, 2, 3, 16, 128), vm(3, 2, 3, 16, 128), vm(3, 2, 3, 8, 128), vm(3, 3, 8, 128),
            vm(2, 16, 128), vm(2, 16, 128), vm(2, 8, 128), vm(8, 128),
            vm(20, 48, 128), vm(20, 32, 128), vm(10, 24, 128), vm(4, 16, 128),
            vm(2, 48, 128), vm(2, 48, 128), vm(2, 24, 128), vm(2, 24, 128), vm(8, 256), vm(2, 8, 256),
            vm(168, 128), vm(136, 128),
            vm(nz, 1, 128), vm(nx * ny, 1, 128),
            pltpu.SemaphoreType.DMA((3,)), pltpu.SemaphoreType.DMA((3,)),
            pltpu.SemaphoreType.DMA((3, 3, 2)), pltpu.SemaphoreType.DMA((3, 3, 2)),
            pltpu.SemaphoreType.DMA((3, 2)), pltpu.SemaphoreType.DMA((3, 2)),
            pltpu.SemaphoreType.DMA((3, 2)), pltpu.SemaphoreType.DMA((3, 2)),
            pltpu.SemaphoreType.DMA((2,)), pltpu.SemaphoreType.DMA((2,)),
        ],
        compiler_params=pltpu.CompilerParams(collective_id=0, has_side_effects=True),
        name="picard",
    )(
        velocity, forcing, phase_block, jnp.asarray(depth_operator()), jnp.asarray(depth_places()),
        prefactor, yield_stress,
    )
    return out[:6] + (out[6].reshape(()),)


def solution(mesh):
    sizes = tuple(mesh.shape[a] for a in ("gx", "gy", "gz"))
    return jax.shard_map(
        functools.partial(per_device, sizes),
        mesh=mesh,
        in_specs=(P(None, "gx", "gy", "gz"), P(None, "gx", "gy", "gz"), P("gx", "gy", "gz"), P(), P()),
        out_specs=(
            P(None, "gx", "gy", "gz"), P("gx", "gy", "gz"), P("gx", "gy", "gz"), P("gx", "gy", "gz"),
            P("gx", "gy", "gz"), P(None, "gx", "gy", "gz"), P(),
        ),
        check_vma=False,
    )
```

time: 234 us -> 51.9 us (0.22)
  the two profiles are of different devices: /device:TPU:8 before, /device:TPU:1 now
where the time goes in v1:
time: 51.9 us; the launch traced here: 51.5 us
  Pallas kernels  43.2 us (83%)
  local copies, waits for them, and re-layouts  5.88 us (11%)
  between operations  2.46 us (5%)
    pallas_call x1, Pallas kernels, per_device(): pl.pallas_call(functools.partial(kernel, sizes), out_shape=(shape(3, 16,...  43.2 us
    unnamed x16, local copies, waits for them, and re-layouts  5.88 us

profile of v1, /device:TPU:1, one launch (start us, length us, event | category | flops | bytes accessed | tf_op | source)
XLA Modules:
  0.0 51.5 jit_solution(11847932405338568253)
XLA Ops:
  0.6 43.2 %picard.1 = (f32[3,16,32,128]{3,2,1,0:T(8,128)}, f32[16,32,128]{2,1,0:T(8,128)}, f32[8,16,64]{2,1,0:T(8,128)}, f32[4,8,32]{2,1,0:T(8,128)}, f32[2,4,16]{2,1,0:T(...) custom-call(f32[3,16,32,128]{3,2,1,0:T(8,128)} %u_hbm.1, f32[3,16,32,128]{3,2,1,0:T(8,128)} %f_hbm.1, ...), custom_call_target="tpu_custom_call" | custom-call | tf_op jit(solution)/shard_map/picard/pallas_call | solution.py:540
  43.8 0.0 copy-start.1
  43.9 0.0 copy-start
  43.9 2.1 %copy.21 = f32[3,16,32,128]{3,2,1,0:T(8,128)} copy(f32[3,16,32,128]{3,2,1,0:T(8,128)} %get-tuple-element.28) | data formatting | bytes 1572864
  46.0 0.0 copy-done.1
  46.0 0.0 copy-start.2
  46.0 0.7 %copy.22 = f32[16,32,128]{2,1,0:T(8,128)} copy(f32[16,32,128]{2,1,0:T(8,128)S(1)} %copy-done.1) | data formatting | bytes 524288
  46.7 0.2 copy-done.2
  46.9 0.0 copy-start.3
  46.9 0.6 %copy.23 = f32[8,16,64]{2,1,0:T(8,128)} copy(f32[8,16,64]{2,1,0:T(8,128)S(1)} %copy-done.2) | data formatting | bytes 65536
  47.5 0.1 copy-done.3
  47.6 0.0 copy-start.4
  47.6 0.6 %copy.24 = f32[4,8,32]{2,1,0:T(8,128)} copy(f32[4,8,32]{2,1,0:T(8,128)S(1)} %copy-done.3) | data formatting | bytes 8192
  48.2 0.1 copy-done.4
  48.3 0.6 %copy.25 = f32[2,4,16]{2,1,0:T(4,128)} copy(f32[2,4,16]{2,1,0:T(4,128)S(1)} %copy-done.4) | data formatting | bytes 1024
  48.9 0.0 copy-done
  48.9 0.9 %copy.26 = f32[3,16,32,128]{3,2,1,0:T(8,128)} copy(f32[3,16,32,128]{3,2,1,0:T(8,128)S(1)} %copy-done) | data formatting | bytes 1572864
Async XLA Ops:
  43.8 2.2 %copy-start.1 = (f32[16,32,128]{2,1,0:T(8,128)S(1)}, f32[16,32,128]{2,1,0:T(8,128)}, u32[]{:S(2)}) copy-start(f32[16,32,128]{2,1,0:T(8,128)} %get-tuple-element.29) | copy-start | bytes 786436
  43.9 5.0 %copy-start = (f32[3,16,32,128]{3,2,1,0:T(8,128)S(1)}, f32[3,16,32,128]{3,2,1,0:T(8,128)}, u32[]{:S(2)}) copy-start(f32[3,16,32,128]{3,2,1,0:T(8,128)} %get-tuple-element.33) | copy-start | bytes 2359300
  46.0 0.9 %copy-start.2 = (f32[8,16,64]{2,1,0:T(8,128)S(1)}, f32[8,16,64]{2,1,0:T(8,128)}, u32[]{:S(2)}) copy-start(f32[8,16,64]{2,1,0:T(8,128)} %get-tuple-element.30) | copy-start | bytes 98308
  46.9 0.7 %copy-start.3 = (f32[4,8,32]{2,1,0:T(8,128)S(1)}, f32[4,8,32]{2,1,0:T(8,128)}, u32[]{:S(2)}) copy-start(f32[4,8,32]{2,1,0:T(8,128)} %get-tuple-element.31) | copy-start | bytes 12292
  47.6 0.7 %copy-start.4 = (f32[2,4,16]{2,1,0:T(4,128)S(1)}, f32[2,4,16]{2,1,0:T(4,128)}, u32[]{:S(2)}) copy-start(f32[2,4,16]{2,1,0:T(4,128)} %get-tuple-element.32) | copy-start | bytes 1540

commit v2 on v1

v2 whole, which is shorter than its diff:
```python
import functools

import jax
import jax.numpy as jnp
import numpy as np
from jax import lax
from jax.experimental import pallas as pl
from jax.experimental.pallas import tpu as pltpu
from jax.sharding import PartitionSpec as P

MESH = pl.DeviceIdType.MESH
RELAX = 0.8
F32 = jnp.float32
VG, LG, SG = 7, 7, 7

ROWS = (128, 32, 8)
LANES = ((0, 64), (64, 32), (96, 16))


def depth_operator():
    out = np.zeros((4, 136, 128), np.float32)
    for low_edge in range(2):
        for high_edge in range(2):
            ext = np.eye(128, dtype=np.float64)
            n = 128
            table = out[low_edge * 2 + high_edge]
            first = 0
            for level, (lane, own) in enumerate(LANES):
                n //= 2
                new = np.zeros((n + 2, 128))
                for k in range(-1, n + 1):
                    for offset, weight in ((-1, 1), (0, 3), (1, 3), (2, 1)):
                        i = 2 * k + offset + first
                        if 0 <= i < ext.shape[0]:
                            new[k + 1] += weight / 8 * ext[i]
                if low_edge:
                    new[0] = 0
                if high_edge:
                    new[-1] = 0
                ext, first = new, 1
                table[:128, lane : lane + own] = new[1:-1].T
                table[128 + 2 * level] = new[0]
                table[129 + 2 * level] = new[-1]
    return out


def depth_places():
    sel = np.zeros((16, 128), np.float32)
    for level, (lane, own) in enumerate(LANES):
        sel[1 + 2 * level, lane] = 1
        sel[8 + 2 * level, lane + own - 1] = 1
    return sel


def kernel(
    sizes,
    u_hbm, f_hbm, phase_hbm, op_hbm, sel_hbm, pref_hbm, yield_hbm,
    u2, vis, c1_ref, c2_ref, c3_ref, res, rms_ref,
    u0, u1, frc, fx, fy, fzl, fzh, fze, diag, scale, base, sx, sy, sz,
    cells, xr, yr, ys, zr, zs, vxr, vyr, vys, vzr, vzs,
    ap, t1, t2, t3, cxs, cxr, cys, cyr, czs, czr, bc, opm,
    ar_a, ar_b, phase_ref, sel_ref, pref_ref, yield_ref,
    load_sem, snd, rcv, vsnd, vrcv, csnd, crcv, asnd, arcv,
):
    nx, ny, nz = sizes
    gx, gy, gz = lax.axis_index("gx"), lax.axis_index("gy"), lax.axis_index("gz")
    coords = {"gx": gx, "gy": gy, "gz": gz}
    has = {
        "gx": (gx > 0, gx < nx - 1),
        "gy": (gy > 0, gy < ny - 1),
        "gz": (gz > 0, gz < nz - 1),
    }
    axes = ("gx", "gy", "gz")

    load_u = pltpu.make_async_copy(u_hbm, u0.at[:, 1:17, 8:40, :], load_sem.at[0])
    load_f = pltpu.make_async_copy(f_hbm, frc, load_sem.at[1])
    edge = (gz == 0).astype(jnp.int32) * 2 + (gz == nz - 1).astype(jnp.int32)
    load_op = pltpu.make_async_copy(op_hbm.at[edge], opm, load_sem.at[2])
    load_phase = pltpu.make_async_copy(phase_hbm, phase_ref, load_sem.at[3])
    load_sel = pltpu.make_async_copy(sel_hbm, sel_ref, load_sem.at[4])
    load_pref = pltpu.make_async_copy(pref_hbm, pref_ref, load_sem.at[5])
    load_yield = pltpu.make_async_copy(yield_hbm, yield_ref, load_sem.at[6])
    for load in (load_u, load_phase, load_pref, load_yield, load_f, load_op, load_sel):
        load.start()

    barrier = pltpu.get_barrier_semaphore()

    core, chip = gx % 2, gx // 2
    beside = gx + 1 - 2 * core
    across = gx - 1 + 2 * core
    has_across = (across >= 0) & (across < nx)
    lines = [(gx, (gz + d) % nz) for d in range(1, nz)] + [(beside, (gz + d) % nz) for d in range(nz)]
    plane = [
        (2 * ((chip + dx) % (nx // 2)) + core, (gy + dy) % ny)
        for dx in range(nx // 2) for dy in range(ny) if (dx, dy) != (0, 0)
    ]

    def greet(**there):
        pl.semaphore_signal(barrier, inc=1, device_id=there, device_id_type=MESH)

    @pl.when(has_across)
    def _():
        greet(gx=across)

    for px, pz in lines:
        greet(gx=px, gz=pz)
    for px, py in plane:
        greet(gx=px, gy=py)

    lane = lax.broadcasted_iota(jnp.int32, (8, 128), 1)
    lane32 = lax.broadcasted_iota(jnp.int32, (32, 128), 1)
    sub8 = lax.broadcasted_iota(jnp.int32, (8, 128), 0)

    def copies(axis, lo_src, lo_dst, hi_src, hi_dst, send, recv):
        k = axes.index(axis)
        lo = pltpu.make_async_remote_copy(
            lo_src, lo_dst, send.at[k, 0], recv.at[k, 1],
            device_id={axis: coords[axis] - 1}, device_id_type=MESH)
        hi = pltpu.make_async_remote_copy(
            hi_src, hi_dst, send.at[k, 1], recv.at[k, 0],
            device_id={axis: coords[axis] + 1}, device_id_type=MESH)
        return axis, lo, hi

    def start(pair):
        axis, lo, hi = pair

        @pl.when(has[axis][0])
        def _():
            lo.start()

        @pl.when(has[axis][1])
        def _():
            hi.start()

    def wait(pair):
        axis, lo, hi = pair

        @pl.when(has[axis][0])
        def _():
            lo.wait_send()
            hi.wait_recv()

        @pl.when(has[axis][1])
        def _():
            hi.wait_send()
            lo.wait_recv()

    def field_copies(phase, u):
        s, w = snd.at[phase], rcv.at[phase]
        return (
            copies("gz", zs.at[phase], zr.at[phase, 1], zs.at[phase], zr.at[phase, 0], s, w),
            copies("gx", u.at[:, 1, 8:40, :], xr.at[phase, 1], u.at[:, 16, 8:40, :], xr.at[phase, 0], s, w),
            copies("gy", ys.at[phase, 0], yr.at[phase, 1], ys.at[phase, 1], yr.at[phase, 0], s, w),
        )

    def merged(low, high):
        return jnp.where(lane % 2 == 0, pltpu.roll(high, 127, 1), pltpu.roll(low, 1, 1))

    def ends_of(column, x):
        return jnp.concatenate([pltpu.roll(column, 127 - 8 * x - 2 * t, 1) for t in range(4)], axis=0)

    def along_z(centre, ends):
        up = jnp.where(lane32 == 127, ends, pltpu.roll(centre, 127, 1))
        down = jnp.where(lane32 == 0, ends, pltpu.roll(centre, 1, 1))
        return up, down

    def planes(body, carry=0, G=7):
        def step(i, carry):
            for j in range(G):
                carry = body(1 + i * G + j, carry)
            return carry
        return lax.fori_loop(0, 14 // G, step, carry)

    def pack_rows(phase, u):
        for comp in range(3):
            for x in range(16):
                ys[phase, 0, comp, x : x + 1, :] = u[comp, x + 1, 8:9, :]
                ys[phase, 1, comp, x : x + 1, :] = u[comp, x + 1, 39:40, :]

    def pack_ends(u):
        accs = [jnp.zeros((8, 128), F32) for _ in range(4)]
        for x in range(16):
            for t in range(4):
                i = 4 * x + t
                k = i % 4
                turned = pltpu.roll(u[x + 1, 8 * t + 8 : 8 * t + 16, :], 2 * i + 1, 1)
                accs[k] = jnp.where(lane // 2 == i, turned, accs[k])
        return (accs[0] + accs[1]) + (accs[2] + accs[3])

    def send_field(phase, u, x_sent=False):
        along_z, along_x, along_y = field_copies(phase, u)
        if not x_sent:
            start(along_x)
        pack_rows(phase, u)
        start(along_y)
        for comp in range(3):
            zs[phase, comp] = pack_ends(u.at[comp])
        start(along_z)
        return along_x, along_y, along_z

    load_u.wait()

    pl.semaphore_wait(barrier, len(lines) + len(plane) + has_across.astype(jnp.int32))
    sent = send_field(0, u0)

    for side, there in enumerate((gx == 0, gx == nx - 1)):
        @pl.when(there)
        def _(side=side):
            for phase in range(3):
                xr[phase, side] = jnp.zeros((3, 32, 128), F32)
            vxr[side] = jnp.zeros((32, 128), F32)
            cxr[side] = jnp.zeros((48, 128), F32)

    for side, there in enumerate((gy == 0, gy == ny - 1)):
        @pl.when(there)
        def _(side=side):
            for phase in range(3):
                yr[phase, side] = jnp.zeros((3, 16, 128), F32)
            vyr[side] = jnp.zeros((16, 128), F32)
            cyr[side] = jnp.zeros((24, 128), F32)

    for side, there in enumerate((gz == 0, gz == nz - 1)):
        @pl.when(there)
        def _(side=side):
            for phase in range(3):
                zr[phase, side] = jnp.zeros((3, 8, 128), F32)
            vzr[side] = jnp.zeros((8, 128), F32)
            czr[side] = jnp.zeros((8, 256), F32)

    for u in (u1, u2):
        for x in (0, 17):
            u[:, x, 8:40, :] = jnp.zeros((3, 32, 128), F32)
        u[:, :, 7:8, :] = jnp.zeros((3, 18, 1, 128), F32)
        u[:, :, 40:41, :] = jnp.zeros((3, 18, 1, 128), F32)
    for x in (0, 17):
        vis[x, 8:40, :] = jnp.zeros((32, 128), F32)
    vis[:, 7:8, :] = jnp.zeros((18, 1, 128), F32)
    vis[:, 40:41, :] = jnp.zeros((18, 1, 128), F32)

    ap[:, 0:8, :] = jnp.zeros((20, 8, 128), F32)
    ap[:, 40:48, :] = jnp.zeros((20, 8, 128), F32)
    t1[...] = jnp.zeros(t1.shape, F32)
    t2[...] = jnp.zeros(t2.shape, F32)

    load_phase.wait()
    load_pref.wait()
    load_yield.wait()
    blocks = phase_ref[...].reshape(32, 32)
    row = lax.broadcasted_iota(jnp.int32, (32, 128), 0)
    spread_z = (lane32 // 4 == row).astype(F32)
    r = lax.broadcasted_iota(jnp.int32, (128, 32), 0)
    c = lax.broadcasted_iota(jnp.int32, (128, 32), 1)
    spread_y = ((r // 32) * 8 + (r % 32) // 4 == c).astype(F32)
    for which, table in enumerate((pref_ref, yield_ref)):
        values = jnp.zeros((32, 32), F32)
        for phase in range(8):
            values = jnp.where(blocks == phase, table[phase], values)
        wide = jnp.dot(values, spread_z, precision=lax.Precision.HIGHEST, preferred_element_type=F32)
        cells[which] = jnp.dot(spread_y, wide, precision=lax.Precision.HIGHEST, preferred_element_type=F32)

    for pair in sent:
        wait(pair)
    for comp in range(3):
        u0[comp, 0, 8:40, :] = xr[0, 0, comp]
        u0[comp, 17, 8:40, :] = xr[0, 1, comp]
        for x in range(16):
            u0[comp, x + 1, 7:8, :] = yr[0, 0, comp, x : x + 1, :]
            u0[comp, x + 1, 40:41, :] = yr[0, 1, comp, x : x + 1, :]

    def inv_body(x, carry):
        d = []
        for comp in range(3):
            centre = u0[comp, x + 1, 8:40, :]
            up, down = along_z(centre, ends_of(ends[comp], x))
            d.append((
                u0[comp, x + 2, 8:40, :] - u0[comp, x, 8:40, :],
                u0[comp, x + 1, 9:41, :] - u0[comp, x + 1, 7:39, :],
                up - down,
            ))
        same = d[0][0] * d[0][0] + d[1][1] * d[1][1] + d[2][2] * d[2][2]
        xy, xz, yz = d[0][1] + d[1][0], d[0][2] + d[2][0], d[1][2] + d[2][1]
        off = xy * xy + xz * xz + yz * yz
        vis[x + 1, 8:40, :] = same * 0.125 + off * 0.0625 + 1.0
        return carry

    def law_body(x, carry):
        inv = vis[x + 1, 8:40, :]
        block = pl.ds((x // 4) * 32, 32)
        creep = cells[0, block, :] * jnp.exp(jnp.log(inv) * (-1.0 / 3.0))
        plastic = cells[1, block, :] * (0.5 * lax.rsqrt(inv))
        vis[x + 1, 8:40, :] = jnp.minimum(creep, plastic)
        return carry

    ends = [merged(zr[0, 0, comp], zr[0, 1, comp]) for comp in range(3)]
    vz = copies("gz", vzs, vzr.at[1], vzs, vzr.at[0], vsnd, vrcv)
    vx = copies("gx", vis.at[1, 8:40, :], vxr.at[1], vis.at[16, 8:40, :], vxr.at[0], vsnd, vrcv)
    vy = copies("gy", vys.at[0], vyr.at[1], vys.at[1], vyr.at[0], vsnd, vrcv)
    for body in (inv_body, law_body):
        body(0, 0)
        body(15, 0)
    start(vx)
    planes(inv_body, G=VG)
    planes(law_body, G=LG)
    for x in range(16):
        vys[0, x : x + 1, :] = vis[x + 1, 8:9, :]
        vys[1, x : x + 1, :] = vis[x + 1, 39:40, :]
    start(vy)
    vzs[...] = pack_ends(vis)
    start(vz)
    vsent = (vx, vy, vz)

    def everywhere(body, carry=0, G=7):
        return planes(body, body(15, body(0, carry)), G)

    flag = {a: tuple(jnp.where(h, 1.0, 0.0).astype(F32) for h in has[a]) for a in axes}

    def weighted(get, k, count):
        total = None
        for offset, weight in ((-1, 0.125), (0, 0.375), (1, 0.375), (2, 0.125)):
            i = 2 * k + offset
            if 0 <= i < count:
                term = get(i) * weight
                total = term if total is None else total + term
        return total

    at = 0
    prev = None
    for level, own in enumerate((8, 4, 2)):
        for k in range(-1, own + 1):
            if level == 0:
                value = weighted(lambda i: vis[i + 1, 8:40, :], k, 16)
            else:
                value = None
                for offset, weight in ((-1, 0.125), (0, 0.375), (1, 0.375), (2, 0.125)):
                    i = 2 * k + offset + 1
                    if 0 <= i < prev[1]:
                        term = ap[prev[0] + i, 8:40, :] * weight
                        value = term if value is None else value + term
            if k == -1:
                value = value * flag["gx"][0]
            if k == own:
                value = value * flag["gx"][1]
            ap[at + k + 1, 8:40, :] = value
        prev = (at, own + 2)
        at += own + 2

    def halve(src, start, rows):
        return (
            (src[:, pl.ds(5, rows, stride=2), :] + src[:, pl.ds(8, rows, stride=2), :])
            + 3.0 * (src[:, pl.ds(6, rows, stride=2), :] + src[:, pl.ds(7, rows, stride=2), :])
        ) * 0.125

    low_y, high_y = flag["gy"]
    t1[:, 7:25, :] = halve(ap, 5, 18)
    t1[:, 7:8, :] = t1[:, 7:8, :] * low_y
    t1[:, 24:25, :] = t1[:, 24:25, :] * high_y
    t2[:, 7:17, :] = halve(t1.at[10:20], 5, 10)
    t2[:, 7:8, :] = t2[:, 7:8, :] * low_y
    t2[:, 16:17, :] = t2[:, 16:17, :] * high_y
    t3[:, 7:13, :] = halve(t2.at[6:10], 5, 6)
    t3[:, 7:8, :] = t3[:, 7:8, :] * low_y
    t3[:, 12:13, :] = t3[:, 12:13, :] * high_y

    levels = ((t1, 0, 8, 16, 0, 0), (t2, 0, 4, 8, 24, 8), (t3, 0, 2, 4, 40, 16))
    for t, _, own, rows, at, _ in levels:
        cxs[0, at : at + rows + 2, :] = t[0, 7 : rows + 9, :]
        cxs[1, at : at + rows + 2, :] = t[own + 1, 7 : rows + 9, :]
    cx = copies("gx", cxs.at[0], cxr.at[1], cxs.at[1], cxr.at[0], csnd, crcv)
    start(cx)

    load_f.wait()
    ends_only = jnp.where((lane32 == 0) | (lane32 == 127), 0.5, 0.0).astype(F32)

    def face_body(x, carry):
        half = 0.5 * vis[x + 1, 8:40, :]
        faces = [
            half + 0.5 * vis[x, 8:40, :],
            half + 0.5 * vis[x + 2, 8:40, :],
            half + 0.5 * vis[x + 1, 7:39, :],
            half + 0.5 * vis[x + 1, 9:41, :],
            half + jnp.where(lane32 == 0, 0.0, pltpu.roll(half, 1, 1)),
            half + jnp.where(lane32 == 127, 0.0, pltpu.roll(half, 127, 1)),
        ]
        fx[x] = faces[0]
        fx[x + 1] = faces[1]
        fy[0, x] = faces[2]
        fy[1, x] = faces[3]
        fzl[x] = faces[4]
        fzh[x] = faces[5]
        diag[x] = ((faces[0] + faces[1]) + (faces[2] + faces[3])) + (faces[4] + faces[5])
        return carry

    def around(u, x, faces):
        total = faces[0] * u[x, 8:40, :] + faces[1] * u[x + 2, 8:40, :]
        return total + (faces[2] * u[x + 1, 7:39, :] + faces[3] * u[x + 1, 9:41, :])

    def faces_of(x):
        return [fx[x], fx[x + 1], fy[0, x], fy[1, x], fzl[x], fzh[x]]

    def first_base(x, carry):
        faces = faces_of(x)
        for comp in range(3):
            centre = u0[comp, x + 1, 8:40, :]
            up, down = along_z(centre, ends_of(ends[comp], x))
            total = around(u0.at[comp], x, faces) + (faces[4] * down + faces[5] * up)
            base[comp, x] = frc[comp, x] + total
        return carry

    everywhere(face_body)
    everywhere(first_base)

    for pair in vsent:
        wait(pair)
    vends = merged(vzr[0], vzr[1])

    def beside_y(row, side):
        return jnp.where(sub8 == (7 if side else 0), row, 0.0)

    def first_end(x, carry):
        extra_z = ends_only * ends_of(vends, x)
        extra = extra_z
        rows = [0.5 * beside_y(vyr[side, pl.ds(x, 1), :], side) for side in (0, 1)]
        nothing = jnp.zeros((16, 128), F32)
        extra = extra + jnp.concatenate([rows[0], nothing, rows[1]], axis=0)
        plane_x = None
        if isinstance(x, int) and x in (0, 15):
            side = x // 15
            plane_x = 0.5 * vxr[side]
            extra = extra + plane_x
        d = diag[x] + extra
        diag[x] = d
        s = RELAX / d
        scale[x] = s
        low, high = fzl[x], fzh[x]
        end = jnp.where(lane32 == 0, low, jnp.where(lane32 == 127, high, 0.0)) + extra_z
        fze[x] = end
        sz[x] = end * s
        fzl[x] = jnp.where(lane32 == 0, 0.0, low)
        fzh[x] = jnp.where(lane32 == 127, 0.0, high)
        low_y = fy[0, x, 0:8, :] + rows[0]
        high_y = fy[1, x, 24:32, :] + rows[1]
        fy[0, x, 0:8, :] = low_y
        fy[1, x, 24:32, :] = high_y
        sy[0, x] = jnp.where(sub8 == 0, low_y * s[0:8], 0.0)
        sy[1, x] = jnp.where(sub8 == 7, high_y * s[24:32], 0.0)
        if plane_x is not None:
            face = fx[x + side] + plane_x
            fx[x + side] = face
            sx[side] = face * s
        for comp in range(3):
            total = base[comp, x] + extra_z * ends_of(ends[comp], x)
            total = total + jnp.concatenate([
                rows[0] * row_of(0, 0, comp, x), nothing, rows[1] * row_of(0, 1, comp, x)], axis=0)
            if plane_x is not None:
                total = total + plane_x * xr[0, side, comp]
            u1[comp, x + 1, 8:40, :] = (1.0 - RELAX) * u0[comp, x + 1, 8:40, :] + s * total
        return carry

    def row_of(phase, side, comp, x):
        return yr[phase, side, comp, pl.ds(x, 1), :]

    def sweep_base(u, x):
        faces = faces_of(x)
        out = []
        for comp in range(3):
            centre = u[comp, x + 1, 8:40, :]
            total = around(u.at[comp], x, faces)
            total = total + (faces[4] * pltpu.roll(centre, 1, 1) + faces[5] * pltpu.roll(centre, 127, 1))
            out.append((centre, frc[comp, x] + total))
        return out

    def added(phase, ends, comp, x, value, z_face, y_faces, x_faces):
        value = value + z_face * ends_of(ends[comp], x)
        value = jnp.concatenate([
            value[0:8] + y_faces[0] * row_of(phase, 0, comp, x),
            value[8:24],
            value[24:32] + y_faces[1] * row_of(phase, 1, comp, x),
        ], axis=0)
        if isinstance(x, int) and x in (0, 15):
            value = value + x_faces[x // 15] * xr[phase, x // 15, comp]
        return value

    first_end(0, 0)
    first_end(15, 0)
    start(field_copies(1, u1)[1])
    planes(first_end, G=SG)
    sent = send_field(1, u1, True)

    wait(cx)
    for t, _, own, rows, at, _ in levels:
        t[1, 7 : rows + 9, :] = t[1, 7 : rows + 9, :] + cxr[0, at : at + rows + 2, :]
        t[own, 7 : rows + 9, :] = t[own, 7 : rows + 9, :] + cxr[1, at : at + rows + 2, :]
    for t, _, own, rows, _, at in levels:
        for k in range(own):
            cys[0, at + k : at + k + 1, :] = t[k + 1, 7:8, :]
            cys[1, at + k : at + k + 1, :] = t[k + 1, rows + 8 : rows + 9, :]
    cy = copies("gy", cys.at[0], cyr.at[1], cys.at[1], cyr.at[0], csnd, crcv)
    start(cy)

    def second_base(x, carry):
        s = scale[x]
        for comp, (centre, total) in enumerate(sweep_base(u1, x)):
            base[comp, x] = (1.0 - RELAX) * centre + s * total
        return carry

    everywhere(second_base)

    for pair in sent:
        wait(pair)
    ends1 = [merged(zr[1, 0, comp], zr[1, 1, comp]) for comp in range(3)]

    def second_end(x, carry):
        for comp in range(3):
            u2[comp, x + 1, 8:40, :] = added(
                1, ends1, comp, x, base[comp, x], sz[x], (sy[0, x], sy[1, x]), (sx[0], sx[1]))
        return carry

    second_end(0, 0)
    second_end(15, 0)
    start(field_copies(2, u2)[1])
    planes(second_end)
    sent = send_field(2, u2, True)

    wait(cy)
    at = 0
    for t, _, own, rows, _, place in levels:
        for k in range(own):
            value = t[k + 1, 8 : rows + 8, :]
            r = lax.broadcasted_iota(jnp.int32, (rows, 128), 0)
            value = value + jnp.where(r == 0, cyr[0, place + k : place + k + 1, :], 0.0)
            value = value + jnp.where(r == rows - 1, cyr[1, place + k : place + k + 1, :], 0.0)
            bc[at : at + rows, :] = value
            at += rows
    load_op.wait()
    load_sel.wait()
    czs[...] = jnp.zeros((8, 256), F32)
    czs[:, 0:168] = lax.dot_general(
        opm[128:136, :], bc[...], (((1,), (1,)), ((), ())),
        precision=lax.Precision.HIGHEST, preferred_element_type=F32)
    cz = copies("gz", czs, czr.at[1], czs, czr.at[0], csnd, crcv)
    start(cz)

    def resid_base(x, carry):
        d = diag[x]
        for comp, (centre, total) in enumerate(sweep_base(u2, x)):
            base[comp, x] = total - d * centre
        return carry

    everywhere(resid_base)

    for pair in sent:
        wait(pair)
    ends2 = [merged(zr[2, 0, comp], zr[2, 1, comp]) for comp in range(3)]

    def resid_end(x, acc):
        low_y = jnp.where(sub8 == 0, fy[0, x, 0:8, :], 0.0)
        high_y = jnp.where(sub8 == 7, fy[1, x, 24:32, :], 0.0)
        for comp in range(3):
            left = added(2, ends2, comp, x, base[comp, x], fze[x], (low_y, high_y), (fx[0], fx[16]))
            res[comp, x] = left
            square = left * left
            acc = acc + ((square[0:8] + square[8:16]) + (square[16:24] + square[24:32]))
        return acc

    acc = everywhere(resid_end, jnp.zeros((8, 128), F32))

    place = core * nz + gz
    ar_a[place] = jnp.sum(acc, axis=0, keepdims=True)
    for px, pz in lines:
        pltpu.make_async_remote_copy(
            ar_a.at[place], ar_a.at[place], asnd.at[0], arcv.at[0],
            device_id={"gx": px, "gz": pz}, device_id_type=MESH).start()

    wait(cz)
    got = jnp.concatenate([czr[0], czr[1]], axis=0)[:, 0:168]
    coarse = jnp.dot(bc[...], opm[0:128, :], precision=lax.Precision.HIGHEST, preferred_element_type=F32)
    coarse = coarse + lax.dot_general(
        got, sel_ref[...], (((0,), (0,)), ((), ())),
        precision=lax.Precision.HIGHEST, preferred_element_type=F32)
    c1_ref[...] = coarse[0:128, 0:64].reshape(8, 16, 64)
    c2_ref[...] = coarse[128:160, 64:96].reshape(4, 8, 32)
    c3_ref[0] = coarse[160:164, 96:112]
    c3_ref[1] = coarse[164:168, 96:112]

    def whole(buf, n, sem):
        return pltpu.make_async_copy(buf.at[0:n], buf.at[0:n], sem)

    whole(ar_a, len(lines), asnd.at[0]).wait()
    whole(ar_a, len(lines), arcv.at[0]).wait()
    mine = chip * ny + gy
    ar_b[mine] = jnp.sum(ar_a[...], axis=0)
    for px, py in plane:
        pltpu.make_async_remote_copy(
            ar_b.at[mine], ar_b.at[mine], asnd.at[1], arcv.at[1],
            device_id={"gx": px, "gy": py}, device_id_type=MESH).start()
    whole(ar_b, len(plane), asnd.at[1]).wait()
    whole(ar_b, len(plane), arcv.at[1]).wait()
    total = jnp.sum(ar_b[...], axis=0)
    cells_all = float(3 * 16 * nx * 32 * ny * 128 * nz)
    rms_ref[...] = jnp.sqrt(jnp.sum(total, axis=1, keepdims=True) / cells_all)


def store(u2, vis, c1, c2, c3, res, rms, smooth_hbm, visc_hbm, c1_hbm, c2_hbm, c3_hbm, resid_hbm, rms_hbm, sem):
    pairs = [(u2.at[comp, x + 1 : x + 9, 8:40, :], smooth_hbm.at[comp, x : x + 8]) for comp in range(3) for x in (0, 8)]
    pairs += [(res.at[comp, x : x + 8], resid_hbm.at[comp, x : x + 8]) for comp in range(3) for x in (0, 8)]
    pairs += [(vis.at[x + 1 : x + 9, 8:40, :], visc_hbm.at[x : x + 8]) for x in (0, 8)]
    pairs += [(c1, c1_hbm), (c2, c2_hbm), (c3, c3_hbm), (rms, rms_hbm)]
    copies = [pltpu.make_async_copy(a, b, sem.at[i]) for i, (a, b) in enumerate(pairs)]
    for copy in copies:
        copy.start()
    for copy in copies:
        copy.wait()


def per_device(sizes, velocity, forcing, phase_block, prefactor, yield_stress):
    nx, ny, nz = sizes
    vm = lambda *shape: pltpu.VMEM(shape, F32)
    any_, hbm, vmem = (pl.BlockSpec(memory_space=s) for s in (pl.ANY, pltpu.HBM, pltpu.VMEM))
    shape = lambda *s: jax.ShapeDtypeStruct(s, F32)
    out = pl.pallas_call(
        functools.partial(kernel, sizes),
        out_shape=(
            vm(3, 18, 48, 128), vm(18, 48, 128), vm(8, 16, 64), vm(4, 8, 32), vm(2, 4, 16),
            vm(3, 16, 32, 128), vm(1, 1),
        ),
        in_specs=[hbm] * 7,
        out_specs=(vmem,) * 7,
        scratch_shapes=[
            vm(3, 18, 48, 128), vm(3, 18, 48, 128), vm(3, 16, 32, 128),
            vm(17, 32, 128), vm(2, 16, 32, 128), vm(16, 32, 128), vm(16, 32, 128), vm(16, 32, 128),
            vm(16, 32, 128), vm(16, 32, 128), vm(3, 16, 32, 128), vm(2, 32, 128), vm(2, 16, 8, 128), vm(16, 32, 128),
            vm(2, 128, 128), vm(3, 2, 3, 32, 128), vm(3, 2, 3, 16, 128), vm(3, 2, 3, 16, 128), vm(3, 2, 3, 8, 128), vm(3, 3, 8, 128),
            vm(2, 32, 128), vm(2, 16, 128), vm(2, 16, 128), vm(2, 8, 128), vm(8, 128),
            vm(20, 48, 128), vm(20, 32, 128), vm(10, 24, 128), vm(4, 16, 128),
            vm(2, 48, 128), vm(2, 48, 128), vm(2, 24, 128), vm(2, 24, 128), vm(8, 256), vm(2, 8, 256),
            vm(168, 128), vm(136, 128),
            vm(2 * nz, 1, 128), vm(nx // 2 * ny, 1, 128),
            pltpu.VMEM((4, 8, 32), jnp.int32), vm(16, 128), pltpu.SMEM((8,), F32), pltpu.SMEM((8,), F32),
            pltpu.SemaphoreType.DMA((7,)),
            pltpu.SemaphoreType.DMA((3, 3, 2)), pltpu.SemaphoreType.DMA((3, 3, 2)),
            pltpu.SemaphoreType.DMA((3, 2)), pltpu.SemaphoreType.DMA((3, 2)),
            pltpu.SemaphoreType.DMA((3, 2)), pltpu.SemaphoreType.DMA((3, 2)),
            pltpu.SemaphoreType.DMA((2,)), pltpu.SemaphoreType.DMA((2,)),
        ],
        compiler_params=pltpu.CompilerParams(collective_id=0, has_side_effects=True, vmem_limit_bytes=60 << 20),
        name="picard",
    )(
        velocity, forcing, phase_block, jnp.asarray(depth_operator()), jnp.asarray(depth_places()),
        prefactor, yield_stress,
    )
    out = pl.pallas_call(
        store,
        out_shape=(
            shape(3, 16, 32, 128), shape(16, 32, 128), shape(8, 16, 64), shape(4, 8, 32), shape(2, 4, 16),
            shape(3, 16, 32, 128), shape(1, 1),
        ),
        in_specs=[vmem] * 7,
        out_specs=(any_,) * 7,
        scratch_shapes=[pltpu.SemaphoreType.DMA((18,))],
        compiler_params=pltpu.CompilerParams(vmem_limit_bytes=1 << 20),
        name="store",
    )(*out)
    return out[:6] + (out[6].reshape(()),)


def solution(mesh):
    sizes = tuple(mesh.shape[a] for a in ("gx", "gy", "gz"))
    return jax.shard_map(
        functools.partial(per_device, sizes),
        mesh=mesh,
        in_specs=(P(None, "gx", "gy", "gz"), P(None, "gx", "gy", "gz"), P("gx", "gy", "gz"), P(), P()),
        out_specs=(
            P(None, "gx", "gy", "gz"), P("gx", "gy", "gz"), P("gx", "gy", "gz"), P("gx", "gy", "gz"),
            P("gx", "gy", "gz"), P(None, "gx", "gy", "gz"), P(),
        ),
        check_vma=False,
    )
```

time: 51.9 us -> 39.6 us (0.76)
  local copies, waits for them, and re-layouts: 5.88 us -> 0 us
  Pallas kernels: 43.2 us -> 38.9 us
  between operations: 2.46 us -> 0.64 us
    unnamed x16 -> x0, local copies, waits for them, and re-layouts: 5.88 us -> none
    pallas_call x1 -> x2, Pallas kernels: 43.2 us -> 38.9 us  [the longest x1 36.9 us: per_device(): pl.pallas_call(functools.partial(kernel, sizes), out_shape=(vm(3, 18, 48,...]
where the time goes in v2:
time: 39.6 us; the launch traced here: 39.5 us
  Pallas kernels  38.9 us (98%)
  between operations  0.64 us (2%)
    pallas_call x1, Pallas kernels, per_device(): pl.pallas_call(functools.partial(kernel, sizes), out_shape=(vm(3, 18, 48,...  36.9 us
    pallas_call x1, Pallas kernels, per_device(): pl.pallas_call(store, out_shape=(shape(3, 16, 32, 128), shape(16, 32, 128...  2.03 us

profile of v2, /device:TPU:1, one launch (start us, length us, event | category | flops | bytes accessed | tf_op | source)
XLA Modules:
  0.0 39.5 jit_solution(7627560463109759605)
XLA Ops:
  0.6 36.9 %picard.1 = (f32[3,18,48,128]{3,2,1,0:T(8,128)S(1)}, f32[18,48,128]{2,1,0:T(8,128)S(1)}, f32[8,16,64]{2,1,0:T(8,128)S(1)}, f32[4,8,32]{2,1,0:T(8,128)S(1)}, f32[...) custom-call(f32[3,16,32,128]{3,2,1,0:T(8,128)} %u_hbm.1, f32[3,16,32,128]{3,2,1,0:T(8,128)} %f_hbm.1, ...), custom_call_target="tpu_custom_call" | custom-call | tf_op jit(solution)/shard_map/picard/pallas_call | solution.py:620
  37.5 2.0 %store.1 = (f32[3,16,32,128]{3,2,1,0:T(8,128)}, f32[16,32,128]{2,1,0:T(8,128)}, f32[8,16,64]{2,1,0:T(8,128)}, f32[4,8,32]{2,1,0:T(8,128)}, f32[2,4,16]{2,1,0:T(4...) custom-call(f32[3,18,48,128]{3,2,1,0:T(8,128)S(1)} %get-tuple-element.21.u2, ...), custom_call_target="tpu_custom_call" | custom-call | tf_op jit(solution)/shard_map/store/pallas_call | solution.py:651
